TPU v7x, 256 devices: a whole 4x4x8 slice. The times are simulated.
256 devices in a mesh: band: 4 (over x_lo, core), fft: 64 (over y, z, x_hi).
Axes of the slice: x: 4 (x_hi: 2, x_lo: 2; x = x_hi * 2 + x_lo), y: 4, z: 8, core: 2. Of those that a mesh axis runs over, the one named last changes fastest.
Arguments:
- orbitals: bfloat16 [16, 2, 262144], P('band', None, 'fft'), may hold values from -6 to 6
- sphere_slot: int32 [262144], P('fft'), may hold values from 0 to 24575, as said below
- stick_column: int32 [8192], P('fft'), may hold values from 0 to 36863, as said below
- potential: float32 [192, 192, 192], P('fft'), may hold values from -3 to 3
- subspace: bfloat16 [64, 2, 262144], P('band', None, 'fft'), may hold values from -0.0234375 to 0.0234375
- previous: bfloat16 [16, 2, 262144], P('band', None, 'fft'), may hold values from -6 to 6
Outputs:
- applied: bfloat16 [16, 2, 262144], P('band', None, 'fft')
- intersection: float32 [2, 64, 16], P(None, 'fft', 'band')
Inputs may be any that keep to these rules, and one draw needn't show every extreme that they name: `sphere_slot`: within each aligned block of 4096 entries the values are distinct. `stick_column`: aligned block d of 128 entries holds distinct columns x * 192 + y with d * 3 <= x < (d + 1) * 3.
All inputs are finite; a program needn't handle non-finite values.
Results may differ from a plain program's by a relative error of at most 0.012.
Values may be sent and summed in bfloat16 or wider, within the bound.
No kernel may reach another device: no remote copies, remote signals or barrier semaphores. Data moves between devices by JAX's collectives and lax.ppermute only.
A program may use at most 64 MiB of HBM per device.

v0:
```python
import functools
import math

import jax
import jax.numpy as jnp
import numpy as np
from jax import lax
from jax.experimental import pallas as pl
from jax.experimental.pallas import tpu as pltpu
from jax.sharding import PartitionSpec as P


BF = jnp.bfloat16
F32 = jnp.float32
N = 192
OWN = 64
DEP = N // OWN
STK = 128
W = 256
EXT = 8
NT = (((1,), (1,)), ((), ()))
TN = (((0,), (0,)), ((), ()))


def dot(a, b, dims=(((1,), (0,)), ((), ()))):
    return lax.dot_general(a, b, dims, preferred_element_type=F32)


@functools.cache
def tables():
    def trig(rows, cols, scale):
        angle = (np.outer(rows, cols) % N) * (2.0 * math.pi / N)
        return np.cos(angle) * scale, np.sin(angle) * scale

    nat = np.arange(N)
    dealt = (np.arange(DEP)[:, None] + DEP * np.arange(OWN)[None, :]).reshape(-1)

    def wide(a, rows, cols):
        out = np.zeros((rows, cols))
        out[: a.shape[0], : a.shape[1]] = a
        return out

    def left(rows, cols, scale, sign, width):
        c, s = trig(rows, cols, scale)
        c, s = wide(c, N, width), wide(s * sign, N, width)
        return np.block([[c, -s], [s, c]])

    def right(rows, cols, scale, sign, height, width):
        c, s = trig(rows, cols, scale)
        c, s = wide(c, height, width), wide(s * sign, height, width)
        return np.block([[c, s], [-s, c]])

    inv = 1.0 / N
    out = {
        "zf": left(dealt, nat, 1.0, 1.0, W),
        "yf": right(nat, nat, 1.0, 1.0, W, W),
        "xf": left(nat, dealt, 1.0, 1.0, N),
        "xi": left(dealt, nat, inv, -1.0, N),
        "yi": right(nat, nat, inv, -1.0, W, W),
        "zi": right(dealt, nat, inv, -1.0, N, W),
    }
    return {k: v.astype(np.float32).astype(BF) for k, v in out.items()}


def iota(shape, dim):
    return lax.broadcasted_iota(jnp.int32, shape, dim)


def column_coords(col):
    c = col.astype(F32)
    x = jnp.floor((c + 0.5) * (1.0 / N))
    return x, c - x * N


def pack_kernel(orb_ref, slot_ref, col_ref, zf_ref, out_ref, a_scr, b_scr):
    npw = slot_ref.shape[1]
    slot = slot_ref[...]
    low = slot & 63
    high = ((slot >> 6) & 1) * W + (slot >> 7)
    half = 1024
    for i in range(0, npw, half):
        cut = slice(i, i + half)
        a_scr[:, cut] = jnp.where(iota((2 * W, half), 0) == high[:, cut], 1.0, 0.0).astype(BF)
        hit = iota((64, half), 0) == low[:, cut]
        for j in range(8):
            row = orb_ref[j // 2, j % 2 : j % 2 + 1, cut].astype(F32)
            b_scr[64 * j : 64 * (j + 1), cut] = jnp.where(hit, row, 0.0).astype(BF)
    grid = dot(b_scr[...], a_scr[...], NT).astype(BF)
    rows = []
    for b in range(4):
        for h in range(2):
            rows.append(
                jnp.concatenate(
                    [grid[64 * (2 * b + p) : 64 * (2 * b + p + 1), W * h : W * (h + 1)] for p in range(2)],
                    axis=1,
                )
            )
    stick = jnp.concatenate(rows, axis=0)
    wave = dot(zf_ref[...], stick, NT)
    x, y = column_coords(col_ref[...])
    xl = x - DEP * jnp.floor((x + 0.5) * (1.0 / DEP))
    ext = jnp.where(iota((EXT, STK), 0) == 0, xl, jnp.where(iota((EXT, STK), 0) == 1, y, 0.0))
    parts = [jnp.broadcast_to(ext[e : e + 1, :], (OWN, STK)) for e in range(EXT)]
    for r in range(DEP):
        for b in range(4):
            for p in range(2):
                base = p * N + r * OWN
                parts.append(wave[base : base + OWN, STK * b : STK * (b + 1)])
    out_ref[...] = jnp.swapaxes(jnp.stack(parts, axis=0), 0, 1).astype(BF)


def plane_kernel(
    in_ref, ext_ref, pot_ref, yf_ref, xf_ref, xi_ref, yi_ref, out_ref, rt_scr, oh_scr, lhs_scr, f_scr, pot_scr
):
    rows = 8 * DEP
    rt_scr[...] = jnp.swapaxes(in_ref[...].astype(F32), 0, 1)
    pot_scr[...] = jnp.zeros(pot_scr.shape, F32)
    pot_scr[:, :, :N] = pot_ref[...]
    sub = iota((8, STK), 0)

    def scatter(g, carry):
        at = pl.multiple_of(g * 8, 8)
        xl = rt_scr[0, pl.ds(at, 8), :]
        y = rt_scr[1, pl.ds(at, 8), :].astype(jnp.int32)
        for d in range(8):
            oh_scr[g, :, STK * d : STK * (d + 1)] = jnp.where(iota((W, STK), 0) == y[d : d + 1, :], 1.0, 0.0).astype(BF)
        for k in range(DEP):
            for row in range(0, rows, 2):
                v = [jnp.where(xl == k, rt_scr[EXT + row + t, pl.ds(at, 8), :], 0.0) for t in range(2)]
                for d in range(8):
                    block = jnp.concatenate([jnp.where(sub == d, u, 0.0) for u in v], axis=0).astype(BF)
                    base = (k * rows + row) * 8
                    lhs_scr[base : base + 16, STK * d : STK * (d + 1)] = block
        res = dot(lhs_scr[...], oh_scr[g], NT)
        for k in range(DEP):
            for row in range(rows):
                base = (k * rows + row) * 8
                f_scr[row // 2, pl.ds(pl.multiple_of(k * OWN + at, 8), 8), (row % 2) * W : (row % 2 + 1) * W] = res[
                    base : base + 8
                ]
        return carry

    lax.fori_loop(0, 8, scatter, 0)

    def plane(r, carry):
        at = r * 4
        a = f_scr[pl.ds(at, 4)].reshape(4 * N, 2 * W).astype(BF)
        ay = dot(a, yf_ref[...]).astype(BF).reshape(4, N, 2 * W)
        stacked = jnp.concatenate(
            [jnp.concatenate([ay[b, :, p * W : (p + 1) * W] for p in range(2)], axis=0) for b in range(4)], axis=1
        )
        ax = dot(xf_ref[...], stacked)
        pot = pot_scr[r]
        pot = jnp.concatenate([jnp.concatenate([pot, pot], axis=0)] * 4, axis=1)
        bx = dot(xi_ref[...], (ax * pot).astype(BF)).astype(BF)
        lined = jnp.concatenate(
            [
                jnp.concatenate([bx[p * N : (p + 1) * N, b * W : (b + 1) * W] for p in range(2)], axis=1)
                for b in range(4)
            ],
            axis=0,
        )
        by = dot(lined, yi_ref[...])
        f_scr[pl.ds(at, 4)] = by.reshape(4, N, 2 * W)
        return carry

    lax.fori_loop(0, DEP, plane, 0)

    def gather(g, carry):
        at = pl.multiple_of(g * 8, 8)
        xl = rt_scr[0, pl.ds(at, 8), :]
        blocks = []
        for k in range(DEP):
            for row in range(rows):
                blocks.append(
                    f_scr[row // 2, pl.ds(pl.multiple_of(k * OWN + at, 8), 8), (row % 2) * W : (row % 2 + 1) * W]
                )
        lhs = jnp.concatenate(blocks, axis=0).astype(BF)
        res = dot(lhs, oh_scr[g])
        keep = [xl == k for k in range(DEP)]
        for row in range(rows):
            total = jnp.zeros((8, STK), F32)
            for k in range(DEP):
                base = (k * rows + row) * 8
                one = jnp.zeros((8, STK), F32)
                for d in range(8):
                    one = jnp.where(sub == d, res[base : base + 8, STK * d : STK * (d + 1)], one)
                total = jnp.where(keep[k], one, total)
            rt_scr[EXT + row, pl.ds(at, 8), :] = total
        return carry

    lax.fori_loop(0, 8, gather, 0)
    e = ext_ref[...]
    hi = e.astype(BF).astype(F32)
    mid = (e - hi).astype(BF).astype(F32)
    lo = e - hi - mid
    rt_scr[0] = hi
    rt_scr[1] = mid
    rt_scr[2] = lo
    out_ref[...] = jnp.swapaxes(rt_scr[...], 0, 1).astype(BF)


def fold_kernel(in_ref, out_ref):
    e = jnp.swapaxes(in_ref[:, :EXT, :].astype(F32), 0, 1)
    out_ref[...] = jnp.sum(e[0] + e[1] + e[2], axis=0, keepdims=True)


def wave_kernel(in_ref, orb_ref, slot_ref, col_ref, zi_ref, out_ref):
    npw = slot_ref.shape[1]
    rt = jnp.swapaxes(in_ref[...].astype(F32), 0, 1)
    cols = []
    for b in range(4):
        cols.append(
            jnp.concatenate([rt[EXT + r * 8 + 2 * b + p] for p in range(2) for r in range(DEP)], axis=0)
        )
    spectrum = jnp.concatenate(cols, axis=1).astype(BF)
    sticks = dot(spectrum, zi_ref[...], TN).astype(BF)
    x, y = column_coords(col_ref[...])
    x = jnp.where(x >= N // 2, x - N, x)
    y = jnp.where(y >= N // 2, y - N, y)
    square = x * x + y * y
    square = jnp.sum(jnp.where(iota((STK, STK), 0) == iota((STK, STK), 1), square, 0.0), axis=1, keepdims=True)
    half = 512

    def pick(i, carry):
        at = pl.multiple_of(i * half, half)
        slot = slot_ref[:, pl.ds(at, half)]
        z = slot >> 7
        hot = jnp.where(iota((W, half), 0) == z, 1.0, 0.0).astype(BF)
        hit = iota((STK, half), 0) == (slot & (STK - 1))
        fz = jnp.where(z >= N // 2, z - N, z).astype(F32)
        kinetic = (fz * fz + jnp.sum(jnp.where(hit, square, 0.0), axis=0, keepdims=True)) * (2.0 / (N * N))
        lines = []
        for p in range(2):
            res = dot(sticks[:, p * W : (p + 1) * W], hot)
            for b in range(4):
                lines.append(
                    jnp.sum(jnp.where(hit, res[b * STK : (b + 1) * STK], 0.0), axis=0, keepdims=True)
                )
        for b in range(4):
            for p in range(2):
                coeff = orb_ref[b, p : p + 1, pl.ds(at, half)].astype(F32)
                lines[p * 4 + b] = lines[p * 4 + b] + kinetic * coeff
        for b in range(4):
            done = jnp.concatenate([lines[b], lines[4 + b]], axis=0)
            out_ref[b, :, pl.ds(at, half)] = done.astype(BF)
        return carry

    lax.fori_loop(0, npw // half, pick, 0)


def overlap_kernel(sub_ref, *refs):
    out_ref = refs[-1]
    sub = sub_ref[...].astype(F32)
    sub = jnp.concatenate([sub[:, 0], sub[:, 1]], axis=1).astype(BF)
    rows = []
    for ref in refs[:-1]:
        prev = ref[...].astype(F32)
        re, im = prev[:, 0], prev[:, 1]
        rows.append(jnp.concatenate([re, im], axis=1))
        rows.append(jnp.concatenate([im, -re], axis=1))
    res = dot(sub, jnp.concatenate(rows, axis=0).astype(BF), NT)
    out_ref[...] = jnp.zeros(out_ref.shape, F32)
    for s in range(4):
        out_ref[16 * s : 16 * (s + 1), :8] = res[:, 8 * s : 8 * (s + 1)]


def call(kernel, outs, scratch, *args):
    return pl.pallas_call(
        kernel,
        out_shape=outs,
        scratch_shapes=scratch,
        compiler_params=pltpu.CompilerParams(vmem_limit_bytes=56 << 20),
    )(*args)


def stage_pack(orb, slot, col):
    npw = slot.shape[1]
    return call(
        pack_kernel,
        jax.ShapeDtypeStruct((OWN, EXT + 8 * DEP, STK), BF),
        [pltpu.VMEM((2 * W, npw), BF), pltpu.VMEM((512, npw), BF)],
        orb, slot, col, jnp.asarray(tables()["zf"]),
    )


def stage_plane(got, ext, pot):
    t = tables()
    return call(
        plane_kernel,
        jax.ShapeDtypeStruct((OWN, EXT + 8 * DEP, STK), BF),
        [
            pltpu.VMEM((EXT + 8 * DEP, OWN, STK), F32),
            pltpu.VMEM((8, W, 8 * STK), BF),
            pltpu.VMEM((8 * 8 * DEP * DEP, 8 * STK), BF),
            pltpu.VMEM((4 * DEP, N, 2 * W), F32),
            pltpu.VMEM((DEP, N, W), F32),
        ],
        got, ext, pot, *[jnp.asarray(t[k]) for k in ("yf", "xf", "xi", "yi")],
    )


def stage_wave(got, orb, slot, col):
    return call(
        wave_kernel,
        jax.ShapeDtypeStruct(orb.shape, BF),
        [],
        got, orb, slot, col, jnp.asarray(tables()["zi"]),
    )


def per_device(orbitals, sphere_slot, stick_column, potential, subspace, previous):
    npw = sphere_slot.shape[0]
    slot = sphere_slot.reshape(1, npw)
    col = stick_column.reshape(1, STK)
    send = stage_pack(orbitals, slot, col)
    got = lax.all_to_all(send, "fft", 0, 0, tiled=True)
    others = [lax.ppermute(previous, "band", [(g, (g + k) % 4) for g in range(4)]) for k in (1, 2, 3)]
    shape = jax.ShapeDtypeStruct((OWN, STK), F32)
    ext = call(overlap_kernel, shape, [], subspace, previous, *others)
    back = stage_plane(got, ext, potential)
    back = lax.all_to_all(back, "fft", 0, 0, tiled=True)
    total = call(fold_kernel, jax.ShapeDtypeStruct((1, STK), F32), [], back)
    moves = [
        (OWN * g + 16 * k + r, OWN * ((g - k) % 4) + 16 * g + r)
        for g in range(4)
        for k in range(4)
        for r in range(16)
    ]
    total = lax.ppermute(total, ("band", "fft"), moves)
    applied = stage_wave(back, orbitals, slot, col)
    return applied, total[:, :8].reshape(2, 1, 4)


def solution(mesh):
    return jax.shard_map(
        per_device,
        mesh=mesh,
        in_specs=(
            P("band", None, "fft"),
            P("fft"),
            P("fft"),
            P("fft", None, None),
            P("band", None, "fft"),
            P("band", None, "fft"),
        ),
        out_specs=(P("band", None, "fft"), P(None, "fft", "band")),
        check_vma=False,
    )
```

profile of v0, /device:TPU:2, one launch (start us, length us, event | category | flops | bytes accessed | tf_op | source)
XLA Modules:
  0.0 93.9 jit_solution(11941634027186355081)
XLA Ops:
  0.6 4.6 %shard_map.131 = bf16[64,32,128]{2,1,0:T(8,128)(2,1)} custom-call(bf16[4,2,4096]{2,1,0:T(2,128)(2,1)} %orb_ref.3, s32[1,4096]{1,0:T(1,128)} %bitcast.3, s32[1,128]{1,0:T(1,128)} %bitcast.5, bf16[384,512]{1,0:T(8,128)(2,1)} %constant.12.clone.zf_ref), custom_call_target="tpu_custom_call" | custom-call | tf_op jit(solution)/shard_map/pallas_call | solution.py:269
  5.3 0.0 copy-start.1
  5.3 13.8 %all-to-all-start = ((bf16[64,32,128]{2,1,0:T(8,128)(2,1)}), bf16[64,32,128]{2,1,0:T(8,128)(2,1)S(1)}, u32[]{:S(2)}, u32[]{:S(2)}) async-start(bf16[64,32,128]{2,1,0:T(8,128)(2,1)} %shard_map.131), calls=%async_computation | async-start | bytes 1048576 | tf_op jit(solution)/shard_map/all_to_all | solution.py:317
  19.1 0.0 copy-done.1
  19.1 0.1 collective-permute-start
  19.2 1.5 %collective-permute-start.1 = (bf16[4,2,4096]{2,1,0:T(2,128)(2,1)S(1)}, bf16[4,2,4096]{2,1,0:T(2,128)(2,1)S(1)}, u32[]{:S(2)}, u32[]{:S(2)}) collective-permute-start(bf16[4,2,4096]{2,1,0:T(2,128)(2,1)S(1)} %copy-done.1), channel_id=1, source_target_pairs={{0,128},{64,192},{128,0},{192,64},{1,129},{65,193},{129,1},{193,65... | collective-permute-start | bytes 196616 | tf_op jit(solution)/shard_map/ppermute | solution.py:318
  20.7 1.4 %collective-permute-start.2 = (bf16[4,2,4096]{2,1,0:T(2,128)(2,1)S(1)}, bf16[4,2,4096]{2,1,0:T(2,128)(2,1)S(1)}, u32[]{:S(2)}, u32[]{:S(2)}) collective-permute-start(bf16[4,2,4096]{2,1,0:T(2,128)(2,1)S(1)} %copy-done.1), channel_id=1, source_target_pairs={{0,192},{64,0},{128,64},{192,128},{1,193},{65,1},{129,65},{193,129... | collective-permute-start | bytes 196616 | tf_op jit(solution)/shard_map/ppermute | solution.py:318
  22.1 1.4 %collective-permute-done.refs_1_ = bf16[4,2,4096]{2,1,0:T(2,128)(2,1)S(1)} collective-permute-done((bf16[4,2,4096]{2,1,0:T(2,128)(2,1)S(1)}, bf16[4,2,4096]{2,1,0:T(2,128)(2,1)S(1)}, u32[]{:S(2)}, u32[]{:S(2)}) %collective-permute-start) | collective-permute-done | bytes 65568 | tf_op jit(solution)/shard_map/ppermute | solution.py:318
  23.5 0.0 copy-start.2
  23.5 1.9 %collective-permute-done.1.refs_2_ = bf16[4,2,4096]{2,1,0:T(2,128)(2,1)S(1)} collective-permute-done((bf16[4,2,4096]{2,1,0:T(2,128)(2,1)S(1)}, bf16[4,2,4096]{2,1,0:T(2,128)(2,1)S(1)}, u32[]{:S(2)}, u32[]{:S(2)}) %collective-permute-start.1) | collective-permute-done | bytes 65568 | tf_op jit(solution)/shard_map/ppermute | solution.py:318
  25.3 0.0 copy-start.3
  25.3 0.7 collective-permute-done.2.refs_3_
  26.1 0.0 copy-done.2
  26.1 0.0 copy-done.3
  26.1 0.0 copy-start.4
  26.1 0.6 copy-done.4
  26.7 2.4 %shard_map.132.ext_ref = f32[64,128]{1,0:T(8,128)} custom-call(bf16[16,2,4096]{2,1,0:T(2,128)(2,1)} %sub_ref.1, bf16[4,2,4096]{2,1,0:T(2,128)(2,1)} %refs_0_.1, bf16[4,2,4096]{2,1,0:T(2,128)(2,1)} %copy-done.2, bf16[4,2,4096]{2,1,0:T(2,128)(2,1)} %copy-done.3, bf16[4,2,4096]{2,1,0:T(2,128)(2,1)} %copy-done.4), custom_call_target="tpu_custom_call" | custom-call | tf_op jit(solution)/shard_map/pallas_call | solution.py:269
  29.1 9.1 %all-to-all-done.in_ref = bf16[64,32,128]{2,1,0:T(8,128)(2,1)S(1)} async-done(((bf16[64,32,128]{2,1,0:T(8,128)(2,1)}), bf16[64,32,128]{2,1,0:T(8,128)(2,1)S(1)}, u32[]{:S(2)}, u32[]{:S(2)}) %all-to-all-start) | async-done | bytes 524320 | tf_op jit(solution)/shard_map/all_to_all | solution.py:317
  38.2 0.0 copy-start
  38.2 0.8 copy-done
  39.0 17.4 %shard_map.133 = bf16[64,32,128]{2,1,0:T(8,128)(2,1)} custom-call(bf16[64,32,128]{2,1,0:T(8,128)(2,1)} %copy-done, f32[64,128]{1,0:T(8,128)} %shard_map.132.ext_ref, f32[3,192,192]{2,1,0:T(8,128)} %pot_ref.1, bf16[512,512]{1,0:T(8,128)(2,1)} %constant.13.clone.yf_ref, bf16[384,384]{1,0:T(8,128)(2,1)} %constant.14.clone.xf_ref, ...), custom_call_target="tpu_custom_call" | custom-call | tf_op jit(solution)/shard_map/pallas_call | solution.py:269
  56.4 24.9 %all_to_all.10.in_ref = bf16[64,32,128]{2,1,0:T(8,128)(2,1)} all-to-all(bf16[64,32,128]{2,1,0:T(8,128)(2,1)} %shard_map.133), channel_id=1, replica_groups=mesh['band'=4,'fft'=64] {'fft'}, dimensions={0} | all-to-all | bytes 1048576 | tf_op jit(solution)/shard_map/all_to_all | solution.py:322
  81.3 1.6 %shard_map.135 = f32[1,128]{1,0:T(1,128)} custom-call(bf16[64,32,128]{2,1,0:T(8,128)(2,1)} %all_to_all.10.in_ref), custom_call_target="tpu_custom_call" | custom-call | tf_op jit(solution)/shard_map/pallas_call | solution.py:269
  82.9 3.9 %collective-permute-start.3 = (f32[1,128]{1,0:T(1,128)}, f32[1,128]{1,0:T(1,128)S(1)}, u32[]{:S(2)}, u32[]{:S(2)}) collective-permute-start(f32[1,128]{1,0:T(1,128)} %shard_map.135), channel_id=1, source_target_pairs={{0,0},{1,1},{2,2},{3,3},{4,4},{5,5},{6,6},{7,7},{8,8},{9,9},{10,10... | collective-permute-start | bytes 1544 | tf_op jit(solution)/shard_map/ppermute | solution.py:330
  86.9 6.4 %shard_map.134 = bf16[4,2,4096]{2,1,0:T(2,128)(2,1)} custom-call(bf16[64,32,128]{2,1,0:T(8,128)(2,1)} %all_to_all.10.in_ref, bf16[4,2,4096]{2,1,0:T(2,128)(2,1)} %orb_ref.3, s32[1,4096]{1,0:T(1,128)} %bitcast.4, s32[1,128]{1,0:T(1,128)} %bitcast.6, bf16[384,512]{1,0:T(8,128)(2,1)} %constant.17.clone.zi_ref), custom_call_target="tpu_custom_call" | custom-call | tf_op jit(solution)/shard_map/pallas_call | solution.py:269
  93.2 0.0 collective-permute-done.3
  93.3 0.6 reshape.15
  (1 shorter events, 0.0 us)
Async XLA Ops:
  5.3 13.8 %copy-start.1 = (bf16[4,2,4096]{2,1,0:T(2,128)(2,1)S(1)}, bf16[4,2,4096]{2,1,0:T(2,128)(2,1)}, u32[]{:S(2)}) copy-start(bf16[4,2,4096]{2,1,0:T(2,128)(2,1)} %refs_0_.1) | copy-start | bytes 196612
  5.3 32.9 %all-to-all-start = ((bf16[64,32,128]{2,1,0:T(8,128)(2,1)}), bf16[64,32,128]{2,1,0:T(8,128)(2,1)S(1)}, u32[]{:S(2)}, u32[]{:S(2)}) async-start(bf16[64,32,128]{2,1,0:T(8,128)(2,1)} %shard_map.131), calls=%async_computation | async-start | bytes 1048576 | tf_op jit(solution)/shard_map/all_to_all | solution.py:317
  19.1 4.4 %collective-permute-start = (bf16[4,2,4096]{2,1,0:T(2,128)(2,1)S(1)}, bf16[4,2,4096]{2,1,0:T(2,128)(2,1)S(1)}, u32[]{:S(2)}, u32[]{:S(2)}) collective-permute-start(bf16[4,2,4096]{2,1,0:T(2,128)(2,1)S(1)} %copy-done.1), channel_id=1, source_target_pairs={{0,64},{64,128},{128,192},{192,0},{1,65},{65,129},{129,193},{193,1... | collective-permute-start | bytes 196616 | tf_op jit(solution)/shard_map/ppermute | solution.py:318
  19.2 6.2 %collective-permute-start.1 = (bf16[4,2,4096]{2,1,0:T(2,128)(2,1)S(1)}, bf16[4,2,4096]{2,1,0:T(2,128)(2,1)S(1)}, u32[]{:S(2)}, u32[]{:S(2)}) collective-permute-start(bf16[4,2,4096]{2,1,0:T(2,128)(2,1)S(1)} %copy-done.1), channel_id=1, source_target_pairs={{0,128},{64,192},{128,0},{192,64},{1,129},{65,193},{129,1},{193,65... | collective-permute-start | bytes 196616 | tf_op jit(solution)/shard_map/ppermute | solution.py:318
  20.7 5.4 %collective-permute-start.2 = (bf16[4,2,4096]{2,1,0:T(2,128)(2,1)S(1)}, bf16[4,2,4096]{2,1,0:T(2,128)(2,1)S(1)}, u32[]{:S(2)}, u32[]{:S(2)}) collective-permute-start(bf16[4,2,4096]{2,1,0:T(2,128)(2,1)S(1)} %copy-done.1), channel_id=1, source_target_pairs={{0,192},{64,0},{128,64},{192,128},{1,193},{65,1},{129,65},{193,129... | collective-permute-start | bytes 196616 | tf_op jit(solution)/shard_map/ppermute | solution.py:318
  23.5 2.6 %copy-start.2 = (bf16[4,2,4096]{2,1,0:T(2,128)(2,1)}, bf16[4,2,4096]{2,1,0:T(2,128)(2,1)S(1)}, u32[]{:S(2)}) copy-start(bf16[4,2,4096]{2,1,0:T(2,128)(2,1)S(1)} %collective-permute-done.refs_1_) | copy-start | bytes 196612
  25.3 0.8 copy-start.3
  26.1 0.6 copy-start.4
  38.2 0.8 copy-start
  82.9 10.4 %collective-permute-start.3 = (f32[1,128]{1,0:T(1,128)}, f32[1,128]{1,0:T(1,128)S(1)}, u32[]{:S(2)}, u32[]{:S(2)}) collective-permute-start(f32[1,128]{1,0:T(1,128)} %shard_map.135), channel_id=1, source_target_pairs={{0,0},{1,1},{2,2},{3,3},{4,4},{5,5},{6,6},{7,7},{8,8},{9,9},{10,10... | collective-permute-start | bytes 1544 | tf_op jit(solution)/shard_map/ppermute | solution.py:330
where the time goes:
time: 94.4 us; the launch traced here: 93.9 us
  Pallas kernels  32.5 us (34%)
  blocking collectives  24.9 us (26%)
  starting transfers between devices  20.7 us (22%)
  waiting for transfers between devices  13.1 us (14%)
  local copies, waits for them, and re-layouts  2.1 us (2%)
    pallas_call x5, Pallas kernels, call(): pl.pallas_call(kernel, out_shape=outs, scratch_shapes=scratch, compiler_p...  32.5 us
    all_to_all x1, blocking collectives, per_device(): back = lax.all_to_all(back, 'fft', 0, 0, tiled=True)  24.9 us
    all_to_all x1, starting transfers between devices, per_device(): got = lax.all_to_all(send, 'fft', 0, 0, tiled=True)  13.8 us
    all_to_all x1, waiting for transfers between devices, per_device(): got = lax.all_to_all(send, 'fft', 0, 0, tiled=True)  9.08 us
    ppermute x3, waiting for transfers between devices, per_device(): lax.ppermute(previous, 'band', [(g, (g + k) % 4) for g in range(4)])  4.02 us
    ppermute x1, starting transfers between devices, per_device(): total = lax.ppermute(total, ('band', 'fft'), moves)  3.94 us
    ppermute x3, starting transfers between devices, per_device(): lax.ppermute(previous, 'band', [(g, (g + k) % 4) for g in range(4)])  2.97 us
  transfers between devices with their start and end apart: 5, of which 4 were waited for; matrix products, arithmetic and copies ran while one was open for 0% of the time, Pallas kernels for 9%

commit v1 on v0

--- a/solution.py
+++ b/solution.py
@@ -18,6 +18,7 @@
 STK = 128
 W = 256
 EXT = 8
+MSG = EXT + 8 * DEP
 NT = (((1,), (1,)), ((), ()))
 TN = (((0,), (0,)), ((), ()))
 
@@ -72,7 +73,7 @@
     return x, c - x * N
 
 
-def pack_kernel(orb_ref, slot_ref, col_ref, zf_ref, out_ref, a_scr, b_scr):
+def pack_kernel(orb_ref, slot_ref, col_ref, zf_ref, out_ref, a_scr, b_scr, m_scr):
     npw = slot_ref.shape[1]
     slot = slot_ref[...]
     low = slot & 63
@@ -100,59 +101,68 @@
     x, y = column_coords(col_ref[...])
     xl = x - DEP * jnp.floor((x + 0.5) * (1.0 / DEP))
     ext = jnp.where(iota((EXT, STK), 0) == 0, xl, jnp.where(iota((EXT, STK), 0) == 1, y, 0.0))
-    parts = [jnp.broadcast_to(ext[e : e + 1, :], (OWN, STK)) for e in range(EXT)]
     for r in range(DEP):
-        for b in range(4):
-            for p in range(2):
-                base = p * N + r * OWN
-                parts.append(wave[base : base + OWN, STK * b : STK * (b + 1)])
-    out_ref[...] = jnp.swapaxes(jnp.stack(parts, axis=0), 0, 1).astype(BF)
+        for j in range(8):
+            base = (j % 2) * N + r * OWN
+            m_scr[r, pl.ds(j, OWN, stride=8), :] = wave[base : base + OWN, STK * (j // 2) : STK * (j // 2 + 1)]
+    parts = [jnp.broadcast_to(ext[None], (OWN, EXT, STK))] + [m_scr[r].reshape(OWN, 8, STK) for r in range(DEP)]
+    out_ref[...] = jnp.concatenate(parts, axis=1).astype(BF)
 
 
 def plane_kernel(
-    in_ref, ext_ref, pot_ref, yf_ref, xf_ref, xi_ref, yi_ref, out_ref, rt_scr, oh_scr, lhs_scr, f_scr, pot_scr
+    in_ref, ext_ref, pot_hbm, yf_hbm, xf_hbm, xi_hbm, yi_hbm, out_ref, oh_scr, lo_scr, hi_scr, pot_scr, yf, xf, xi, yi, sems
 ):
     rows = 8 * DEP
-    rt_scr[...] = jnp.swapaxes(in_ref[...].astype(F32), 0, 1)
-    pot_scr[...] = jnp.zeros(pot_scr.shape, F32)
-    pot_scr[:, :, :N] = pot_ref[...]
-    sub = iota((8, STK), 0)
-
-    def scatter(g, carry):
-        at = pl.multiple_of(g * 8, 8)
-        xl = rt_scr[0, pl.ds(at, 8), :]
-        y = rt_scr[1, pl.ds(at, 8), :].astype(jnp.int32)
-        for d in range(8):
-            oh_scr[g, :, STK * d : STK * (d + 1)] = jnp.where(iota((W, STK), 0) == y[d : d + 1, :], 1.0, 0.0).astype(BF)
-        for k in range(DEP):
-            for row in range(0, rows, 2):
-                v = [jnp.where(xl == k, rt_scr[EXT + row + t, pl.ds(at, 8), :], 0.0) for t in range(2)]
-                for d in range(8):
-                    block = jnp.concatenate([jnp.where(sub == d, u, 0.0) for u in v], axis=0).astype(BF)
-                    base = (k * rows + row) * 8
-                    lhs_scr[base : base + 16, STK * d : STK * (d + 1)] = block
-        res = dot(lhs_scr[...], oh_scr[g], NT)
-        for k in range(DEP):
-            for row in range(rows):
-                base = (k * rows + row) * 8
-                f_scr[row // 2, pl.ds(pl.multiple_of(k * OWN + at, 8), 8), (row % 2) * W : (row % 2 + 1) * W] = res[
-                    base : base + 8
-                ]
+    copies = [
+        pltpu.make_async_copy(src, dst, sems.at[i])
+        for i, (src, dst) in enumerate(
+            [(yf_hbm, yf), (xf_hbm, xf), (pot_hbm, pot_scr), (xi_hbm, xi), (yi_hbm, yi)]
+        )
+    ]
+    for copy in copies:
+        copy.start()
+    halves = (lo_scr, hi_scr)
+
+    def scatter(i, carry):
+        for u in range(16):
+            d = i * 16 + u
+            m = in_ref[d].astype(F32)
+            xl, y = m[0:1], m[1:2].astype(jnp.int32)
+            hot = jnp.where(iota((N, STK), 0) == y, 1.0, 0.0).astype(BF)
+            hot = jnp.concatenate([hot, jnp.zeros((W - N, STK), BF)], axis=0)
+            oh_scr[d] = hot
+            lhs = jnp.concatenate([jnp.where(xl == k, m[EXT:], 0.0) for k in range(DEP)], axis=0).astype(BF)
+            res = dot(lhs, hot, NT)
+            for k in range(DEP):
+                for r in range(DEP):
+                    base = k * rows + r * 8
+                    for h in range(2):
+                        at = pl.multiple_of((r * N + k * OWN + d) * 8, 8)
+                        halves[h][pl.ds(at, 8), :] = res[
+                            base : base + 8, h * STK : (h + 1) * STK
+                        ]
         return carry
 
-    lax.fori_loop(0, 8, scatter, 0)
+    lax.fori_loop(0, OWN // 16, scatter, 0)
+    for copy in copies:
+        copy.wait()
 
     def plane(r, carry):
-        at = r * 4
-        a = f_scr[pl.ds(at, 4)].reshape(4 * N, 2 * W).astype(BF)
-        ay = dot(a, yf_ref[...]).astype(BF).reshape(4, N, 2 * W)
+        at = r * 8 * N
+        lined = []
+        for b in range(4):
+            parts = [
+                half[pl.ds(at + 2 * b + p, N, stride=8), :].astype(BF) for p in range(2) for half in halves
+            ]
+            lined.append(jnp.concatenate(parts, axis=1))
+        ay = dot(jnp.concatenate(lined, axis=0), yf[...]).astype(BF).reshape(4, N, 2 * W)
         stacked = jnp.concatenate(
             [jnp.concatenate([ay[b, :, p * W : (p + 1) * W] for p in range(2)], axis=0) for b in range(4)], axis=1
         )
-        ax = dot(xf_ref[...], stacked)
-        pot = pot_scr[r]
+        ax = dot(xf[...], stacked)
+        pot = jnp.concatenate([pot_scr[r], jnp.zeros((N, W - N), F32)], axis=1)
         pot = jnp.concatenate([jnp.concatenate([pot, pot], axis=0)] * 4, axis=1)
-        bx = dot(xi_ref[...], (ax * pot).astype(BF)).astype(BF)
+        bx = dot(xi[...], (ax * pot).astype(BF)).astype(BF)
         lined = jnp.concatenate(
             [
                 jnp.concatenate([bx[p * N : (p + 1) * N, b * W : (b + 1) * W] for p in range(2)], axis=1)
@@ -160,44 +170,51 @@
             ],
             axis=0,
         )
-        by = dot(lined, yi_ref[...])
-        f_scr[pl.ds(at, 4)] = by.reshape(4, N, 2 * W)
+        by = dot(lined, yi[...])
+        for b in range(4):
+            for p in range(2):
+                for h in range(2):
+                    halves[h][pl.ds(at + 2 * b + p, N, stride=8), :] = by[
+                        b * N : (b + 1) * N, (2 * p + h) * STK : (2 * p + h + 1) * STK
+                    ]
         return carry
 
     lax.fori_loop(0, DEP, plane, 0)
-
-    def gather(g, carry):
-        at = pl.multiple_of(g * 8, 8)
-        xl = rt_scr[0, pl.ds(at, 8), :]
-        blocks = []
-        for k in range(DEP):
-            for row in range(rows):
-                blocks.append(
-                    f_scr[row // 2, pl.ds(pl.multiple_of(k * OWN + at, 8), 8), (row % 2) * W : (row % 2 + 1) * W]
-                )
-        lhs = jnp.concatenate(blocks, axis=0).astype(BF)
-        res = dot(lhs, oh_scr[g])
-        keep = [xl == k for k in range(DEP)]
-        for row in range(rows):
-            total = jnp.zeros((8, STK), F32)
-            for k in range(DEP):
-                base = (k * rows + row) * 8
-                one = jnp.zeros((8, STK), F32)
-                for d in range(8):
-                    one = jnp.where(sub == d, res[base : base + 8, STK * d : STK * (d + 1)], one)
-                total = jnp.where(keep[k], one, total)
-            rt_scr[EXT + row, pl.ds(at, 8), :] = total
+    spot = iota((EXT, STK), 0)
+
+    def gather(i, carry):
+        for u in range(8):
+            pair = [i * 16 + 2 * u, i * 16 + 2 * u + 1]
+            blocks = []
+            for d in pair:
+                for k in range(DEP):
+                    for r in range(DEP):
+                        blocks.append(
+                            jnp.concatenate(
+                                [
+                                    half[pl.ds(pl.multiple_of((r * N + k * OWN + d) * 8, 8), 8), :]
+                                    for half in halves
+                                ],
+                                axis=1,
+                            )
+                        )
+            lhs = jnp.concatenate(blocks, axis=0).astype(BF)
+            res = dot(lhs, jnp.concatenate([oh_scr[d] for d in pair], axis=1))
+            for t, d in enumerate(pair):
+                xl = in_ref[d, 0:8].astype(F32)[0:1]
+                took = [
+                    res[(t * DEP + k) * rows : (t * DEP + k + 1) * rows, t * STK : (t + 1) * STK] for k in range(DEP)
+                ]
+                field = jnp.where(xl == 0.0, took[0], jnp.where(xl == 1.0, took[1], took[2]))
+                e = ext_ref[pl.ds(d, 1), :]
+                top = e.astype(BF).astype(F32)
+                mid = (e - top).astype(BF).astype(F32)
+                low = e - top - mid
+                head = jnp.where(spot == 0, top, jnp.where(spot == 1, mid, jnp.where(spot == 2, low, 0.0)))
+                out_ref[d] = jnp.concatenate([head, field], axis=0).astype(BF)
         return carry
 
-    lax.fori_loop(0, 8, gather, 0)
-    e = ext_ref[...]
-    hi = e.astype(BF).astype(F32)
-    mid = (e - hi).astype(BF).astype(F32)
-    lo = e - hi - mid
-    rt_scr[0] = hi
-    rt_scr[1] = mid
-    rt_scr[2] = lo
-    out_ref[...] = jnp.swapaxes(rt_scr[...], 0, 1).astype(BF)
+    lax.fori_loop(0, OWN // 16, gather, 0)
 
 
 def fold_kernel(in_ref, out_ref):
@@ -205,16 +222,28 @@
     out_ref[...] = jnp.sum(e[0] + e[1] + e[2], axis=0, keepdims=True)
 
 
-def wave_kernel(in_ref, orb_ref, slot_ref, col_ref, zi_ref, out_ref):
+def wave_kernel(in_ref, orb_ref, slot_ref, col_ref, zi_ref, out_ref, m_scr):
     npw = slot_ref.shape[1]
-    rt = jnp.swapaxes(in_ref[...].astype(F32), 0, 1)
+    for r in range(DEP):
+        m_scr[r] = in_ref[:, EXT + 8 * r : EXT + 8 * (r + 1), :].astype(F32).reshape(OWN * 8, STK)
     cols = []
     for b in range(4):
-        cols.append(
-            jnp.concatenate([rt[EXT + r * 8 + 2 * b + p] for p in range(2) for r in range(DEP)], axis=0)
-        )
+        picks = [m_scr[r, pl.ds(2 * b + p, OWN, stride=8), :] for p in range(2) for r in range(DEP)]
+        cols.append(jnp.concatenate(picks, axis=0))
     spectrum = jnp.concatenate(cols, axis=1).astype(BF)
     sticks = dot(spectrum, zi_ref[...], TN).astype(BF)
+    sticks = [
+        jnp.concatenate(
+            [
+                jnp.concatenate(
+                    [sticks[b * STK + 64 * h : b * STK + 64 * (h + 1), p * W : (p + 1) * W] for h in range(2)], axis=1
+                )
+                for b in range(4)
+            ],
+            axis=0,
+        )
+        for p in range(2)
+    ]
     x, y = column_coords(col_ref[...])
     x = jnp.where(x >= N // 2, x - N, x)
     y = jnp.where(y >= N // 2, y - N, y)
@@ -226,17 +255,20 @@
         at = pl.multiple_of(i * half, half)
         slot = slot_ref[:, pl.ds(at, half)]
         z = slot >> 7
-        hot = jnp.where(iota((W, half), 0) == z, 1.0, 0.0).astype(BF)
-        hit = iota((STK, half), 0) == (slot & (STK - 1))
+        stick = slot & (STK - 1)
+        hot = jnp.concatenate(
+            [jnp.where(iota((W, half), 0) == jnp.where(stick >> 6 == h, z, -1), 1.0, 0.0).astype(BF) for h in range(2)],
+            axis=0,
+        )
+        hit = iota((STK, half), 0) == stick
+        low = iota((64, half), 0) == (stick & 63)
         fz = jnp.where(z >= N // 2, z - N, z).astype(F32)
         kinetic = (fz * fz + jnp.sum(jnp.where(hit, square, 0.0), axis=0, keepdims=True)) * (2.0 / (N * N))
         lines = []
         for p in range(2):
-            res = dot(sticks[:, p * W : (p + 1) * W], hot)
+            res = dot(sticks[p], hot)
             for b in range(4):
-                lines.append(
-                    jnp.sum(jnp.where(hit, res[b * STK : (b + 1) * STK], 0.0), axis=0, keepdims=True)
-                )
+                lines.append(jnp.sum(jnp.where(low, res[b * 64 : (b + 1) * 64], 0.0), axis=0, keepdims=True))
         for b in range(4):
             for p in range(2):
                 coeff = orb_ref[b, p : p + 1, pl.ds(at, half)].astype(F32)
@@ -246,7 +278,7 @@
             out_ref[b, :, pl.ds(at, half)] = done.astype(BF)
         return carry
 
-    lax.fori_loop(0, npw // half, pick, 0)
+    lax.fori_loop(0, npw // half, pick, 0, unroll=2)
 
 
 def overlap_kernel(sub_ref, *refs):
@@ -278,33 +310,36 @@
     npw = slot.shape[1]
     return call(
         pack_kernel,
-        jax.ShapeDtypeStruct((OWN, EXT + 8 * DEP, STK), BF),
-        [pltpu.VMEM((2 * W, npw), BF), pltpu.VMEM((512, npw), BF)],
+        jax.ShapeDtypeStruct((OWN, MSG, STK), BF),
+        [pltpu.VMEM((2 * W, npw), BF), pltpu.VMEM((512, npw), BF), pltpu.VMEM((DEP, OWN * 8, STK), F32)],
         orb, slot, col, jnp.asarray(tables()["zf"]),
     )
 
 
 def stage_plane(got, ext, pot):
     t = tables()
-    return call(
+    names = ("yf", "xf", "xi", "yi")
+    return pl.pallas_call(
         plane_kernel,
-        jax.ShapeDtypeStruct((OWN, EXT + 8 * DEP, STK), BF),
-        [
-            pltpu.VMEM((EXT + 8 * DEP, OWN, STK), F32),
-            pltpu.VMEM((8, W, 8 * STK), BF),
-            pltpu.VMEM((8 * 8 * DEP * DEP, 8 * STK), BF),
-            pltpu.VMEM((4 * DEP, N, 2 * W), F32),
-            pltpu.VMEM((DEP, N, W), F32),
+        out_shape=jax.ShapeDtypeStruct((OWN, MSG, STK), BF),
+        in_specs=[pl.BlockSpec(memory_space=pltpu.VMEM)] * 2 + [pl.BlockSpec(memory_space=pl.ANY)] * 5,
+        scratch_shapes=[
+            pltpu.VMEM((OWN, W, STK), BF),
+            pltpu.VMEM((8 * DEP * N, STK), F32),
+            pltpu.VMEM((8 * DEP * N, STK), F32),
+            pltpu.VMEM((DEP, N, N), F32),
+            *[pltpu.VMEM(t[k].shape, BF) for k in names],
+            pltpu.SemaphoreType.DMA((5,)),
         ],
-        got, ext, pot, *[jnp.asarray(t[k]) for k in ("yf", "xf", "xi", "yi")],
-    )
+        compiler_params=pltpu.CompilerParams(vmem_limit_bytes=56 << 20),
+    )(got, ext, pot, *[jnp.asarray(t[k]) for k in names])
 
 
 def stage_wave(got, orb, slot, col):
     return call(
         wave_kernel,
         jax.ShapeDtypeStruct(orb.shape, BF),
-        [],
+        [pltpu.VMEM((DEP, OWN * 8, STK), F32)],
         got, orb, slot, col, jnp.asarray(tables()["zi"]),
     )
 

time: 94.4 us -> 88.5 us (0.937)
  Pallas kernels: 32.5 us -> 26.6 us
    pallas_call x5 -> x4, Pallas kernels: 32.5 us -> 14.9 us  [call(): pl.pallas_call(kernel, out_shape=outs, scratch_shapes=scratch, compiler_p...]
    pallas_call x0 -> x1, Pallas kernels: none -> 11.8 us  [stage_plane(): pl.pallas_call(plane_kernel, out_shape=jax.ShapeDtypeStruct((OWN, MSG, ST...]
  transfers between devices with their start and end apart: 5 -> 5, of which waited for: 4 -> 4; matrix products, arithmetic and copies ran while one was open for 0% -> 0% of each run, Pallas kernels for 9% -> 10%
where the time goes in v1:
time: 88.5 us; the launch traced here: 88.1 us
  Pallas kernels  26.6 us (30%)
  blocking collectives  24.9 us (28%)
  starting transfers between devices  20.7 us (23%)
  waiting for transfers between devices  13.1 us (15%)
  local copies, waits for them, and re-layouts  2.1 us (2%)
    all_to_all x1, blocking collectives, per_device(): back = lax.all_to_all(back, 'fft', 0, 0, tiled=True)  24.9 us
    pallas_call x4, Pallas kernels, call(): pl.pallas_call(kernel, out_shape=outs, scratch_shapes=scratch, compiler_p...  14.9 us
    all_to_all x1, starting transfers between devices, per_device(): got = lax.all_to_all(send, 'fft', 0, 0, tiled=True)  13.8 us
    pallas_call x1, Pallas kernels, stage_plane(): pl.pallas_call(plane_kernel, out_shape=jax.ShapeDtypeStruct((OWN, MSG, ST...  11.8 us
    all_to_all x1, waiting for transfers between devices, per_device(): got = lax.all_to_all(send, 'fft', 0, 0, tiled=True)  9.08 us
    ppermute x3, waiting for transfers between devices, per_device(): lax.ppermute(previous, 'band', [(g, (g + k) % 4) for g in range(4)])  4.02 us
    ppermute x1, starting transfers between devices, per_device(): total = lax.ppermute(total, ('band', 'fft'), moves)  3.94 us
    ppermute x3, starting transfers between devices, per_device(): lax.ppermute(previous, 'band', [(g, (g + k) % 4) for g in range(4)])  2.97 us
  transfers between devices with their start and end apart: 5, of which 4 were waited for; matrix products, arithmetic and copies ran while one was open for 0% of the time, Pallas kernels for 10%

profile of v1, /device:TPU:2, one launch (start us, length us, event | category | flops | bytes accessed | tf_op | source)
XLA Modules:
  0.0 88.1 jit_solution(10749165311130116872)
XLA Ops:
  0.6 4.6 %shard_map.131 = bf16[64,32,128]{2,1,0:T(8,128)(2,1)} custom-call(bf16[4,2,4096]{2,1,0:T(2,128)(2,1)} %orb_ref.3, s32[1,4096]{1,0:T(1,128)} %bitcast.3, s32[1,128]{1,0:T(1,128)} %bitcast.5, bf16[384,512]{1,0:T(8,128)(2,1)} %constant.12.clone.zf_ref), custom_call_target="tpu_custom_call" | custom-call | tf_op jit(solution)/shard_map/pallas_call | solution.py:301
  5.2 0.0 copy-start.1
  5.2 13.8 %all-to-all-start = ((bf16[64,32,128]{2,1,0:T(8,128)(2,1)}), bf16[64,32,128]{2,1,0:T(8,128)(2,1)S(1)}, u32[]{:S(2)}, u32[]{:S(2)}) async-start(bf16[64,32,128]{2,1,0:T(8,128)(2,1)} %shard_map.131), calls=%async_computation | async-start | bytes 1048576 | tf_op jit(solution)/shard_map/all_to_all | solution.py:352
  19.0 0.0 copy-done.1
  19.1 0.1 collective-permute-start
  19.1 1.5 %collective-permute-start.1 = (bf16[4,2,4096]{2,1,0:T(2,128)(2,1)S(1)}, bf16[4,2,4096]{2,1,0:T(2,128)(2,1)S(1)}, u32[]{:S(2)}, u32[]{:S(2)}) collective-permute-start(bf16[4,2,4096]{2,1,0:T(2,128)(2,1)S(1)} %copy-done.1), channel_id=1, source_target_pairs={{0,128},{64,192},{128,0},{192,64},{1,129},{65,193},{129,1},{193,65... | collective-permute-start | bytes 196616 | tf_op jit(solution)/shard_map/ppermute | solution.py:353
  20.7 1.4 %collective-permute-start.2 = (bf16[4,2,4096]{2,1,0:T(2,128)(2,1)S(1)}, bf16[4,2,4096]{2,1,0:T(2,128)(2,1)S(1)}, u32[]{:S(2)}, u32[]{:S(2)}) collective-permute-start(bf16[4,2,4096]{2,1,0:T(2,128)(2,1)S(1)} %copy-done.1), channel_id=1, source_target_pairs={{0,192},{64,0},{128,64},{192,128},{1,193},{65,1},{129,65},{193,129... | collective-permute-start | bytes 196616 | tf_op jit(solution)/shard_map/ppermute | solution.py:353
  22.0 1.4 %collective-permute-done.refs_1_ = bf16[4,2,4096]{2,1,0:T(2,128)(2,1)S(1)} collective-permute-done((bf16[4,2,4096]{2,1,0:T(2,128)(2,1)S(1)}, bf16[4,2,4096]{2,1,0:T(2,128)(2,1)S(1)}, u32[]{:S(2)}, u32[]{:S(2)}) %collective-permute-start) | collective-permute-done | bytes 65568 | tf_op jit(solution)/shard_map/ppermute | solution.py:353
  23.4 0.0 copy-start.2
  23.4 1.9 %collective-permute-done.1.refs_2_ = bf16[4,2,4096]{2,1,0:T(2,128)(2,1)S(1)} collective-permute-done((bf16[4,2,4096]{2,1,0:T(2,128)(2,1)S(1)}, bf16[4,2,4096]{2,1,0:T(2,128)(2,1)S(1)}, u32[]{:S(2)}, u32[]{:S(2)}) %collective-permute-start.1) | collective-permute-done | bytes 65568 | tf_op jit(solution)/shard_map/ppermute | solution.py:353
  25.3 0.0 copy-start.3
  25.3 0.7 collective-permute-done.2.refs_3_
  26.1 0.0 copy-done.2
  26.1 0.0 copy-done.3
  26.1 0.0 copy-start.4
  26.1 0.6 copy-done.4
  26.7 2.4 %shard_map.132.ext_ref = f32[64,128]{1,0:T(8,128)} custom-call(bf16[16,2,4096]{2,1,0:T(2,128)(2,1)} %sub_ref.1, bf16[4,2,4096]{2,1,0:T(2,128)(2,1)} %refs_0_.1, bf16[4,2,4096]{2,1,0:T(2,128)(2,1)} %copy-done.2, bf16[4,2,4096]{2,1,0:T(2,128)(2,1)} %copy-done.3, bf16[4,2,4096]{2,1,0:T(2,128)(2,1)} %copy-done.4), custom_call_target="tpu_custom_call" | custom-call | tf_op jit(solution)/shard_map/pallas_call | solution.py:301
  29.1 9.1 %all-to-all-done.in_ref = bf16[64,32,128]{2,1,0:T(8,128)(2,1)S(1)} async-done(((bf16[64,32,128]{2,1,0:T(8,128)(2,1)}), bf16[64,32,128]{2,1,0:T(8,128)(2,1)S(1)}, u32[]{:S(2)}, u32[]{:S(2)}) %all-to-all-start) | async-done | bytes 524320 | tf_op jit(solution)/shard_map/all_to_all | solution.py:352
  38.2 0.0 copy-start
  38.2 0.8 copy-done
  39.0 11.8 %shard_map.133 = bf16[64,32,128]{2,1,0:T(8,128)(2,1)} custom-call(bf16[64,32,128]{2,1,0:T(8,128)(2,1)} %copy-done, f32[64,128]{1,0:T(8,128)} %shard_map.132.ext_ref, f32[3,192,192]{2,1,0:T(8,128)} %pot_hbm.1, bf16[512,512]{1,0:T(8,128)(2,1)} %constant.13.clone.yf_hbm, bf16[384,384]{1,0:T(8,128)(2,1)} %constant.14.clone.xf_hbm, ...), custom_call_target="tpu_custom_call" | custom-call | tf_op jit(solution)/shard_map/pallas_call | solution.py:322
  50.7 24.9 %all_to_all.10.in_ref = bf16[64,32,128]{2,1,0:T(8,128)(2,1)} all-to-all(bf16[64,32,128]{2,1,0:T(8,128)(2,1)} %shard_map.133), channel_id=1, replica_groups=mesh['band'=4,'fft'=64] {'fft'}, dimensions={0} | all-to-all | bytes 1048576 | tf_op jit(solution)/shard_map/all_to_all | solution.py:357
  75.6 1.6 %shard_map.135 = f32[1,128]{1,0:T(1,128)} custom-call(bf16[64,32,128]{2,1,0:T(8,128)(2,1)} %all_to_all.10.in_ref), custom_call_target="tpu_custom_call" | custom-call | tf_op jit(solution)/shard_map/pallas_call | solution.py:301
  77.2 3.9 %collective-permute-start.3 = (f32[1,128]{1,0:T(1,128)}, f32[1,128]{1,0:T(1,128)S(1)}, u32[]{:S(2)}, u32[]{:S(2)}) collective-permute-start(f32[1,128]{1,0:T(1,128)} %shard_map.135), channel_id=1, source_target_pairs={{0,0},{1,1},{2,2},{3,3},{4,4},{5,5},{6,6},{7,7},{8,8},{9,9},{10,10... | collective-permute-start | bytes 1544 | tf_op jit(solution)/shard_map/ppermute | solution.py:365
  81.2 6.3 %shard_map.134 = bf16[4,2,4096]{2,1,0:T(2,128)(2,1)} custom-call(bf16[64,32,128]{2,1,0:T(8,128)(2,1)} %all_to_all.10.in_ref, bf16[4,2,4096]{2,1,0:T(2,128)(2,1)} %orb_ref.3, s32[1,4096]{1,0:T(1,128)} %bitcast.4, s32[1,128]{1,0:T(1,128)} %bitcast.6, bf16[384,512]{1,0:T(8,128)(2,1)} %constant.17.clone.zi_ref), custom_call_target="tpu_custom_call" | custom-call | tf_op jit(solution)/shard_map/pallas_call | solution.py:301
  87.5 0.0 collective-permute-done.3
  87.5 0.6 reshape.15
  (1 shorter events, 0.0 us)
Async XLA Ops:
  5.2 13.8 %copy-start.1 = (bf16[4,2,4096]{2,1,0:T(2,128)(2,1)S(1)}, bf16[4,2,4096]{2,1,0:T(2,128)(2,1)}, u32[]{:S(2)}) copy-start(bf16[4,2,4096]{2,1,0:T(2,128)(2,1)} %refs_0_.1) | copy-start | bytes 196612
  5.2 32.9 %all-to-all-start = ((bf16[64,32,128]{2,1,0:T(8,128)(2,1)}), bf16[64,32,128]{2,1,0:T(8,128)(2,1)S(1)}, u32[]{:S(2)}, u32[]{:S(2)}) async-start(bf16[64,32,128]{2,1,0:T(8,128)(2,1)} %shard_map.131), calls=%async_computation | async-start | bytes 1048576 | tf_op jit(solution)/shard_map/all_to_all | solution.py:352
  19.1 4.4 %collective-permute-start = (bf16[4,2,4096]{2,1,0:T(2,128)(2,1)S(1)}, bf16[4,2,4096]{2,1,0:T(2,128)(2,1)S(1)}, u32[]{:S(2)}, u32[]{:S(2)}) collective-permute-start(bf16[4,2,4096]{2,1,0:T(2,128)(2,1)S(1)} %copy-done.1), channel_id=1, source_target_pairs={{0,64},{64,128},{128,192},{192,0},{1,65},{65,129},{129,193},{193,1... | collective-permute-start | bytes 196616 | tf_op jit(solution)/shard_map/ppermute | solution.py:353
  19.1 6.2 %collective-permute-start.1 = (bf16[4,2,4096]{2,1,0:T(2,128)(2,1)S(1)}, bf16[4,2,4096]{2,1,0:T(2,128)(2,1)S(1)}, u32[]{:S(2)}, u32[]{:S(2)}) collective-permute-start(bf16[4,2,4096]{2,1,0:T(2,128)(2,1)S(1)} %copy-done.1), channel_id=1, source_target_pairs={{0,128},{64,192},{128,0},{192,64},{1,129},{65,193},{129,1},{193,65... | collective-permute-start | bytes 196616 | tf_op jit(solution)/shard_map/ppermute | solution.py:353
  20.7 5.4 %collective-permute-start.2 = (bf16[4,2,4096]{2,1,0:T(2,128)(2,1)S(1)}, bf16[4,2,4096]{2,1,0:T(2,128)(2,1)S(1)}, u32[]{:S(2)}, u32[]{:S(2)}) collective-permute-start(bf16[4,2,4096]{2,1,0:T(2,128)(2,1)S(1)} %copy-done.1), channel_id=1, source_target_pairs={{0,192},{64,0},{128,64},{192,128},{1,193},{65,1},{129,65},{193,129... | collective-permute-start | bytes 196616 | tf_op jit(solution)/shard_map/ppermute | solution.py:353
  23.4 2.6 %copy-start.2 = (bf16[4,2,4096]{2,1,0:T(2,128)(2,1)}, bf16[4,2,4096]{2,1,0:T(2,128)(2,1)S(1)}, u32[]{:S(2)}) copy-start(bf16[4,2,4096]{2,1,0:T(2,128)(2,1)S(1)} %collective-permute-done.refs_1_) | copy-start | bytes 196612
  25.3 0.8 copy-start.3
  26.1 0.6 copy-start.4
  38.2 0.8 copy-start
  77.2 10.2 %collective-permute-start.3 = (f32[1,128]{1,0:T(1,128)}, f32[1,128]{1,0:T(1,128)S(1)}, u32[]{:S(2)}, u32[]{:S(2)}) collective-permute-start(f32[1,128]{1,0:T(1,128)} %shard_map.135), channel_id=1, source_target_pairs={{0,0},{1,1},{2,2},{3,3},{4,4},{5,5},{6,6},{7,7},{8,8},{9,9},{10,10... | collective-permute-start | bytes 1544 | tf_op jit(solution)/shard_map/ppermute | solution.py:365

commit v2 on v1

--- a/solution.py
+++ b/solution.py
@@ -17,8 +17,10 @@
 DEP = N // OWN
 STK = 128
 W = 256
-EXT = 8
-MSG = EXT + 8 * DEP
+ROWS = 8 * DEP
+EXT = 2
+MSG = EXT + ROWS
+GRP = 16
 NT = (((1,), (1,)), ((), ()))
 TN = (((0,), (0,)), ((), ()))
 
@@ -73,12 +75,24 @@
     return x, c - x * N
 
 
-def pack_kernel(orb_ref, slot_ref, col_ref, zf_ref, out_ref, a_scr, b_scr, m_scr):
+def fetch(sems, *pairs):
+    copies = [pltpu.make_async_copy(src, dst, sems.at[i]) for i, (src, dst) in enumerate(pairs)]
+    for copy in copies:
+        copy.start()
+    return copies
+
+
+def pack_kernel(
+    orb_hbm, slot_hbm, col_hbm, zf_hbm, out_ref, a_scr, b_scr, m_scr, orb_ref, slot_ref, col_ref, zf_ref, sems
+):
+    copies = fetch(sems, (slot_hbm, slot_ref), (orb_hbm, orb_ref), (col_hbm, col_ref), (zf_hbm, zf_ref))
     npw = slot_ref.shape[1]
+    copies[0].wait()
     slot = slot_ref[...]
     low = slot & 63
     high = ((slot >> 6) & 1) * W + (slot >> 7)
     half = 1024
+    copies[1].wait()
     for i in range(0, npw, half):
         cut = slice(i, i + half)
         a_scr[:, cut] = jnp.where(iota((2 * W, half), 0) == high[:, cut], 1.0, 0.0).astype(BF)
@@ -97,37 +111,43 @@
                 )
             )
     stick = jnp.concatenate(rows, axis=0)
+    copies[2].wait()
+    copies[3].wait()
     wave = dot(zf_ref[...], stick, NT)
     x, y = column_coords(col_ref[...])
     xl = x - DEP * jnp.floor((x + 0.5) * (1.0 / DEP))
-    ext = jnp.where(iota((EXT, STK), 0) == 0, xl, jnp.where(iota((EXT, STK), 0) == 1, y, 0.0))
+    ext = jnp.concatenate([xl, y], axis=0)
     for r in range(DEP):
         for j in range(8):
             base = (j % 2) * N + r * OWN
             m_scr[r, pl.ds(j, OWN, stride=8), :] = wave[base : base + OWN, STK * (j // 2) : STK * (j // 2 + 1)]
-    parts = [jnp.broadcast_to(ext[None], (OWN, EXT, STK))] + [m_scr[r].reshape(OWN, 8, STK) for r in range(DEP)]
-    out_ref[...] = jnp.concatenate(parts, axis=1).astype(BF)
+
+    def pour(i, carry):
+        at = pl.multiple_of(i * GRP * 8, 8)
+        block = [m_scr[r, pl.ds(at, GRP * 8), :] for r in range(DEP)]
+        parts = []
+        for u in range(GRP):
+            parts += [ext] + [block[r][8 * u : 8 * u + 8] for r in range(DEP)]
+        out_ref[pl.ds(pl.multiple_of(i * GRP * MSG, 16), GRP * MSG), :] = jnp.concatenate(parts, axis=0).astype(BF)
+        return carry
+
+    lax.fori_loop(0, OWN // GRP, pour, 0)
 
 
 def plane_kernel(
-    in_ref, ext_ref, pot_hbm, yf_hbm, xf_hbm, xi_hbm, yi_hbm, out_ref, oh_scr, lo_scr, hi_scr, pot_scr, yf, xf, xi, yi, sems
+    in_ref, pot_hbm, yf_hbm, xf_hbm, xi_hbm, yi_hbm, out_ref, oh_scr, xl_scr, lo_scr, hi_scr, pot_scr, yf, xf, xi, yi, sems
 ):
-    rows = 8 * DEP
-    copies = [
-        pltpu.make_async_copy(src, dst, sems.at[i])
-        for i, (src, dst) in enumerate(
-            [(yf_hbm, yf), (xf_hbm, xf), (pot_hbm, pot_scr), (xi_hbm, xi), (yi_hbm, yi)]
-        )
-    ]
-    for copy in copies:
-        copy.start()
+    rows = ROWS
+    copies = fetch(sems, (yf_hbm, yf), (xf_hbm, xf), (pot_hbm, pot_scr), (xi_hbm, xi), (yi_hbm, yi))
     halves = (lo_scr, hi_scr)
 
     def scatter(i, carry):
-        for u in range(16):
-            d = i * 16 + u
-            m = in_ref[d].astype(F32)
+        block = in_ref[pl.ds(pl.multiple_of(i * GRP * MSG, 16), GRP * MSG), :].astype(F32)
+        for u in range(GRP):
+            d = i * GRP + u
+            m = block[MSG * u : MSG * (u + 1)]
             xl, y = m[0:1], m[1:2].astype(jnp.int32)
+            xl_scr[pl.ds(d, 1), :] = xl
             hot = jnp.where(iota((N, STK), 0) == y, 1.0, 0.0).astype(BF)
             hot = jnp.concatenate([hot, jnp.zeros((W - N, STK), BF)], axis=0)
             oh_scr[d] = hot
@@ -143,7 +163,7 @@
                         ]
         return carry
 
-    lax.fori_loop(0, OWN // 16, scatter, 0)
+    lax.fori_loop(0, OWN // GRP, scatter, 0)
     for copy in copies:
         copy.wait()
 
@@ -180,11 +200,11 @@
         return carry
 
     lax.fori_loop(0, DEP, plane, 0)
-    spot = iota((EXT, STK), 0)
 
     def gather(i, carry):
-        for u in range(8):
-            pair = [i * 16 + 2 * u, i * 16 + 2 * u + 1]
+        parts = []
+        for u in range(GRP // 2):
+            pair = [i * GRP + 2 * u, i * GRP + 2 * u + 1]
             blocks = []
             for d in pair:
                 for k in range(DEP):
@@ -201,35 +221,42 @@
             lhs = jnp.concatenate(blocks, axis=0).astype(BF)
             res = dot(lhs, jnp.concatenate([oh_scr[d] for d in pair], axis=1))
             for t, d in enumerate(pair):
-                xl = in_ref[d, 0:8].astype(F32)[0:1]
+                xl = xl_scr[pl.ds(d, 1), :]
                 took = [
                     res[(t * DEP + k) * rows : (t * DEP + k + 1) * rows, t * STK : (t + 1) * STK] for k in range(DEP)
                 ]
                 field = jnp.where(xl == 0.0, took[0], jnp.where(xl == 1.0, took[1], took[2]))
-                e = ext_ref[pl.ds(d, 1), :]
-                top = e.astype(BF).astype(F32)
-                mid = (e - top).astype(BF).astype(F32)
-                low = e - top - mid
-                head = jnp.where(spot == 0, top, jnp.where(spot == 1, mid, jnp.where(spot == 2, low, 0.0)))
-                out_ref[d] = jnp.concatenate([head, field], axis=0).astype(BF)
+                parts += [jnp.zeros((EXT, STK), F32), field]
+        out_ref[pl.ds(pl.multiple_of(i * GRP * MSG, 16), GRP * MSG), :] = jnp.concatenate(parts, axis=0).astype(BF)
         return carry
 
-    lax.fori_loop(0, OWN // 16, gather, 0)
-
-
-def fold_kernel(in_ref, out_ref):
-    e = jnp.swapaxes(in_ref[:, :EXT, :].astype(F32), 0, 1)
-    out_ref[...] = jnp.sum(e[0] + e[1] + e[2], axis=0, keepdims=True)
-
-
-def wave_kernel(in_ref, orb_ref, slot_ref, col_ref, zi_ref, out_ref, m_scr):
+    lax.fori_loop(0, OWN // GRP, gather, 0)
+
+
+def wave_kernel(
+    in_ref, orb_hbm, slot_hbm, col_hbm, zi_hbm, out_ref, sum_ref, m_scr, orb_ref, slot_ref, col_ref, zi_ref, sems
+):
+    copies = fetch(sems, (zi_hbm, zi_ref), (col_hbm, col_ref), (slot_hbm, slot_ref), (orb_hbm, orb_ref))
     npw = slot_ref.shape[1]
-    for r in range(DEP):
-        m_scr[r] = in_ref[:, EXT + 8 * r : EXT + 8 * (r + 1), :].astype(F32).reshape(OWN * 8, STK)
+
+    def unpour(i, total):
+        block = in_ref[pl.ds(pl.multiple_of(i * GRP * MSG, 16), GRP * MSG), :].astype(F32)
+        for u in range(GRP):
+            total = total + block[MSG * u : MSG * u + 1]
+            for r in range(DEP):
+                row = MSG * u + EXT + 8 * r
+                m_scr[r, pl.ds(pl.multiple_of((i * GRP + u) * 8, 8), 8), :] = block[row : row + 8]
+        return total
+
+    total = lax.fori_loop(0, OWN // GRP, unpour, jnp.zeros((1, STK), F32))
+    total = total[:, 0:8] + total[:, 8:16] + total[:, 16:24]
+    sum_ref[...] = jnp.concatenate([total[:, 0:4], total[:, 4:8]], axis=0)
     cols = []
     for b in range(4):
         picks = [m_scr[r, pl.ds(2 * b + p, OWN, stride=8), :] for p in range(2) for r in range(DEP)]
         cols.append(jnp.concatenate(picks, axis=0))
+    for copy in copies:
+        copy.wait()
     spectrum = jnp.concatenate(cols, axis=1).astype(BF)
     sticks = dot(spectrum, zi_ref[...], TN).astype(BF)
     sticks = [
@@ -282,66 +309,98 @@
 
 
 def overlap_kernel(sub_ref, *refs):
-    out_ref = refs[-1]
+    refs, out_refs = refs[:4], refs[4:]
     sub = sub_ref[...].astype(F32)
     sub = jnp.concatenate([sub[:, 0], sub[:, 1]], axis=1).astype(BF)
     rows = []
-    for ref in refs[:-1]:
+    for ref in refs:
         prev = ref[...].astype(F32)
         re, im = prev[:, 0], prev[:, 1]
         rows.append(jnp.concatenate([re, im], axis=1))
         rows.append(jnp.concatenate([im, -re], axis=1))
     res = dot(sub, jnp.concatenate(rows, axis=0).astype(BF), NT)
-    out_ref[...] = jnp.zeros(out_ref.shape, F32)
-    for s in range(4):
-        out_ref[16 * s : 16 * (s + 1), :8] = res[:, 8 * s : 8 * (s + 1)]
-
-
-def call(kernel, outs, scratch, *args):
+    top = res.astype(BF).astype(F32)
+    mid = (res - top).astype(BF).astype(F32)
+    low = res - top - mid
+    pad = jnp.zeros((16, STK - 24), F32)
+    for k in range(4):
+        cut = slice(8 * k, 8 * (k + 1))
+        out_refs[k][...] = jnp.concatenate([top[:, cut], mid[:, cut], low[:, cut], pad], axis=1).astype(BF)
+
+
+def run(kernel, outs, scratch, args, near):
+    space = [pltpu.VMEM if n else pltpu.HBM for n in near]
     return pl.pallas_call(
         kernel,
         out_shape=outs,
+        in_specs=[pl.BlockSpec(memory_space=m) for m in space],
         scratch_shapes=scratch,
-        compiler_params=pltpu.CompilerParams(vmem_limit_bytes=56 << 20),
-    )(*args)
-
-
-def stage_pack(orb, slot, col):
-    npw = slot.shape[1]
-    return call(
+        compiler_params=pltpu.CompilerParams(vmem_limit_bytes=52 << 20),
+    )(*[pltpu.with_memory_space_constraint(a, m) for a, m in zip(args, space)])
+
+
+def like(a):
+    return pltpu.VMEM(a.shape, a.dtype)
+
+
+def stage_pack(*args):
+    args = (*args, jnp.asarray(tables()["zf"]))
+    npw = args[1].shape[1]
+    return run(
         pack_kernel,
-        jax.ShapeDtypeStruct((OWN, MSG, STK), BF),
-        [pltpu.VMEM((2 * W, npw), BF), pltpu.VMEM((512, npw), BF), pltpu.VMEM((DEP, OWN * 8, STK), F32)],
-        orb, slot, col, jnp.asarray(tables()["zf"]),
+        pltpu.VMEM((OWN * MSG, STK), BF),
+        [
+            pltpu.VMEM((2 * W, npw), BF),
+            pltpu.VMEM((512, npw), BF),
+            pltpu.VMEM((DEP, OWN * 8, STK), F32),
+            *map(like, args),
+            pltpu.SemaphoreType.DMA((len(args),)),
+        ],
+        args,
+        (0, 0, 0, 0),
     )
 
 
-def stage_plane(got, ext, pot):
-    t = tables()
-    names = ("yf", "xf", "xi", "yi")
-    return pl.pallas_call(
+def stage_over(sub, prevs):
+    return run(overlap_kernel, [pltpu.VMEM((16, STK), BF)] * 4, [], (sub, *prevs), (1, 1, 1, 1, 1))
+
+
+def stage_plane(got, pot):
+    args = [jnp.asarray(tables()[k]) for k in ("yf", "xf", "xi", "yi")]
+    return run(
         plane_kernel,
-        out_shape=jax.ShapeDtypeStruct((OWN, MSG, STK), BF),
-        in_specs=[pl.BlockSpec(memory_space=pltpu.VMEM)] * 2 + [pl.BlockSpec(memory_space=pl.ANY)] * 5,
-        scratch_shapes=[
+        pltpu.VMEM((OWN * MSG, STK), BF),
+        [
             pltpu.VMEM((OWN, W, STK), BF),
-            pltpu.VMEM((8 * DEP * N, STK), F32),
-            pltpu.VMEM((8 * DEP * N, STK), F32),
-            pltpu.VMEM((DEP, N, N), F32),
-            *[pltpu.VMEM(t[k].shape, BF) for k in names],
+            pltpu.VMEM((OWN, STK), F32),
+            pltpu.VMEM((ROWS * N, STK), F32),
+            pltpu.VMEM((ROWS * N, STK), F32),
+            like(pot),
+            *map(like, args),
             pltpu.SemaphoreType.DMA((5,)),
         ],
-        compiler_params=pltpu.CompilerParams(vmem_limit_bytes=56 << 20),
-    )(got, ext, pot, *[jnp.asarray(t[k]) for k in names])
-
-
-def stage_wave(got, orb, slot, col):
-    return call(
+        (got, pot, *args),
+        (1, 0, 0, 0, 0, 0),
+    )
+
+
+def stage_wave(got, *args):
+    args = (*args, jnp.asarray(tables()["zi"]))
+    order = (args[0], args[1], args[2], args[3])
+    return run(
         wave_kernel,
-        jax.ShapeDtypeStruct(orb.shape, BF),
-        [pltpu.VMEM((DEP, OWN * 8, STK), F32)],
-        got, orb, slot, col, jnp.asarray(tables()["zi"]),
+        (jax.ShapeDtypeStruct(args[0].shape, BF), jax.ShapeDtypeStruct((2, 4), F32)),
+        [pltpu.VMEM((DEP, OWN * 8, STK), F32), *map(like, order), pltpu.SemaphoreType.DMA((len(args),))],
+        (got, *order),
+        (1, 0, 0, 0, 0),
     )
+
+
+def exchange(tiles):
+    return lax.all_to_all(tiles, "fft", 0, 0, tiled=True).reshape(OWN * MSG, STK)
+
+
+TILES = (OWN, MSG // 2, 2, STK)
 
 
 def per_device(orbitals, sphere_slot, stick_column, potential, subspace, previous):
@@ -349,22 +408,18 @@
     slot = sphere_slot.reshape(1, npw)
     col = stick_column.reshape(1, STK)
     send = stage_pack(orbitals, slot, col)
-    got = lax.all_to_all(send, "fft", 0, 0, tiled=True)
-    others = [lax.ppermute(previous, "band", [(g, (g + k) % 4) for g in range(4)]) for k in (1, 2, 3)]
-    shape = jax.ShapeDtypeStruct((OWN, STK), F32)
-    ext = call(overlap_kernel, shape, [], subspace, previous, *others)
-    back = stage_plane(got, ext, potential)
-    back = lax.all_to_all(back, "fft", 0, 0, tiled=True)
-    total = call(fold_kernel, jax.ShapeDtypeStruct((1, STK), F32), [], back)
-    moves = [
-        (OWN * g + 16 * k + r, OWN * ((g - k) % 4) + 16 * g + r)
-        for g in range(4)
-        for k in range(4)
-        for r in range(16)
-    ]
-    total = lax.ppermute(total, ("band", "fft"), moves)
-    applied = stage_wave(back, orbitals, slot, col)
-    return applied, total[:, :8].reshape(2, 1, 4)
+    got = exchange(send.reshape(TILES))
+    shifts = [[(g, (g + k) % 4) for g in range(4)] for k in (1, 2, 3)]
+    others = [lax.ppermute(previous, "band", s) for s in shifts]
+    over = stage_over(subspace, [previous, *others])
+    mine = [over[0]] + [lax.ppermute(over[k], "band", [(b, a) for a, b in shifts[k - 1]]) for k in (1, 2, 3)]
+    field = stage_plane(got, potential)
+    sums = jnp.concatenate([jnp.stack(mine)] * 2)
+    sums = lax.dynamic_slice_in_dim(sums, (4 - lax.axis_index("band")) % 4, 4, 0).reshape(OWN, 1, STK)
+    head = jnp.pad(sums, ((0, 0), (0, 1), (0, 0)))[:, None]
+    back = exchange(lax.dynamic_update_slice(field.reshape(TILES), head, (0, 0, 0, 0)))
+    applied, total = stage_wave(back, orbitals, slot, col)
+    return applied, total.reshape(2, 1, 4)
 
 
 def solution(mesh):

time: 88.5 us -> 76.9 us (0.87)
  Pallas kernels: 26.6 us -> 21.3 us
  blocking collectives: 24.9 us -> 22.1 us
  starting transfers between devices: 20.7 us -> 18.3 us
  local copies, waits for them, and re-layouts: 2.1 us -> 0.14 us
  waiting for transfers between devices: 13.1 us -> 14 us
    pallas_call x5 -> x4, Pallas kernels: 26.6 us -> 21.3 us  [run(): pl.pallas_call(kernel, out_shape=outs, in_specs=[pl.BlockSpec(memory_spac...]
    all_to_all x1, blocking collectives: 24.9 us -> 22.1 us  [exchange(): lax.all_to_all(tiles, 'fft', 0, 0, tiled=True).reshape(OWN * MSG, STK)]
    all_to_all x1, waiting for transfers between devices: 9.08 us -> 11.1 us  [exchange(): lax.all_to_all(tiles, 'fft', 0, 0, tiled=True).reshape(OWN * MSG, STK)]
    all_to_all x1, starting transfers between devices: 13.8 us -> 12.4 us  [exchange(): lax.all_to_all(tiles, 'fft', 0, 0, tiled=True).reshape(OWN * MSG, STK)]
    unnamed x10 -> x11, local copies, waits for them, and re-layouts: 1.43 us -> 0.06 us
    ppermute x4 -> x6, waiting for transfers between devices: 4.02 us -> 2.91 us  [the longest x3 2.9 us: per_device(): lax.ppermute(over[k], 'band', [(b, a) for a, b in shifts[k - 1]])]
    ppermute x4 -> x6, starting transfers between devices: 6.91 us -> 5.89 us  [the longest x3 3.78 us: per_device(): others = [lax.ppermute(previous, 'band', s) for s in shifts]]
  transfers between devices with their start and end apart: 5 -> 7, of which waited for: 4 -> 3; matrix products, arithmetic and copies ran while one was open for 0% -> 0% of each run, Pallas kernels for 10% -> 7%
where the time goes in v2:
time: 76.9 us; the launch traced here: 76.5 us
  blocking collectives  22.1 us (29%)
  Pallas kernels  21.3 us (28%)
  starting transfers between devices  18.3 us (24%)
  waiting for transfers between devices  14 us (18%)
  between operations  0.77 us (1%)
    all_to_all x1, blocking collectives, exchange(): lax.all_to_all(tiles, 'fft', 0, 0, tiled=True).reshape(OWN * MSG, STK)  22.1 us
    pallas_call x4, Pallas kernels, run(): pl.pallas_call(kernel, out_shape=outs, in_specs=[pl.BlockSpec(memory_spac...  21.3 us
    all_to_all x1, starting transfers between devices, exchange(): lax.all_to_all(tiles, 'fft', 0, 0, tiled=True).reshape(OWN * MSG, STK)  12.4 us
    all_to_all x1, waiting for transfers between devices, exchange(): lax.all_to_all(tiles, 'fft', 0, 0, tiled=True).reshape(OWN * MSG, STK)  11.1 us
    ppermute x3, starting transfers between devices, per_device(): others = [lax.ppermute(previous, 'band', s) for s in shifts]  3.78 us
    ppermute x3, waiting for transfers between devices, per_device(): lax.ppermute(over[k], 'band', [(b, a) for a, b in shifts[k - 1]])  2.9 us
    ppermute x3, starting transfers between devices, per_device(): lax.ppermute(over[k], 'band', [(b, a) for a, b in shifts[k - 1]])  2.11 us
  transfers between devices with their start and end apart: 7, of which 3 were waited for; matrix products, arithmetic and copies ran while one was open for 0% of the time, Pallas kernels for 7%

profile of v2, /device:TPU:2, one launch (start us, length us, event | category | flops | bytes accessed | tf_op | source)
XLA Modules:
  0.0 76.5 jit_solution(8731795103452942124)
XLA Ops:
  0.6 0.1 collective-permute-start
  0.7 2.3 %collective-permute-start.1 = (bf16[4,2,4096]{2,1,0:T(2,128)(2,1)}, bf16[4,2,4096]{2,1,0:T(2,128)(2,1)S(1)}, u32[]{:S(2)}, u32[]{:S(2)}) collective-permute-start(bf16[4,2,4096]{2,1,0:T(2,128)(2,1)} %refs_0_.1), channel_id=1, source_target_pairs={{0,128},{64,192},{128,0},{192,64},{1,129},{65,193},{129,1},{193,65... | collective-permute-start | bytes 196616 | tf_op jit(solution)/shard_map/ppermute | solution.py:413
  3.0 1.4 %collective-permute-start.2 = (bf16[4,2,4096]{2,1,0:T(2,128)(2,1)}, bf16[4,2,4096]{2,1,0:T(2,128)(2,1)S(1)}, u32[]{:S(2)}, u32[]{:S(2)}) collective-permute-start(bf16[4,2,4096]{2,1,0:T(2,128)(2,1)} %refs_0_.1), channel_id=1, source_target_pairs={{0,192},{64,0},{128,64},{192,128},{1,193},{65,1},{129,65},{193,129... | collective-permute-start | bytes 196616 | tf_op jit(solution)/shard_map/ppermute | solution.py:413
  4.4 4.5 %shard_map.131 = bf16[1664,128]{1,0:T(8,128)(2,1)} custom-call(bf16[4,2,4096]{2,1,0:T(2,128)(2,1)} %orb_hbm.3, s32[1,4096]{1,0:T(1,128)} %bitcast.27, s32[1,128]{1,0:T(1,128)} %bitcast.30, bf16[384,512]{1,0:T(8,128)(2,1)} %constant.36.clone.zf_hbm), custom_call_target="tpu_custom_call" | custom-call | tf_op jit(solution)/shard_map/pallas_call | solution.py:333
  9.0 0.0 copy-start
  9.0 0.0 copy-start.1
  9.0 12.4 %all-to-all-start = ((bf16[64,13,2,128]{3,2,1,0:T(2,128)(2,1)}), bf16[64,13,2,128]{3,2,1,0:T(2,128)(2,1)S(1)}, u32[]{:S(2)}, u32[]{:S(2)}) async-start(bf16[64,13,2,128]{3,2,1,0:T(2,128)(2,1)} %bitcast.2), calls=%async_computation | async-start | bytes 851968 | tf_op jit(solution)/shard_map/all_to_all | solution.py:400
  21.4 0.0 collective-permute-done.refs_1_
  21.4 0.0 collective-permute-done.1.refs_2_
  21.4 0.0 collective-permute-done.2.refs_3_
  21.4 0.0 copy-done
  21.4 0.0 copy-done.1
  21.5 0.8 %shard_map.133 = (bf16[16,128]{1,0:T(8,128)(2,1)S(1)}, bf16[16,128]{1,0:T(8,128)(2,1)S(1)}, bf16[16,128]{1,0:T(8,128)(2,1)S(1)}, bf16[16,128]{1,0:T(8,128)(2,1)S(1)}) custom-call(bf16[16,2,4096]{2,1,0:T(2,128)(2,1)S(1)} %copy-done, bf16[4,2,4096]{2,1,0:T(2,128)(2,1)S(1)} %copy-done.1, bf16[4,2,4096]{2,1,0:T(2,128)(2,1)S(1)} %collective-permute-done.refs_1_, ...), custom_call_target="tpu_custom_call" | custom-call | tf_op jit(solution)/shard_map/pallas_call | solution.py:333
  22.2 0.4 collective-permute-start.3
  22.6 1.6 %collective-permute-start.4 = (bf16[16,128]{1,0:T(8,128)(2,1)S(1)}, bf16[16,128]{1,0:T(8,128)(2,1)S(1)}, u32[]{:S(2)}, u32[]{:S(2)}) collective-permute-start(bf16[16,128]{1,0:T(8,128)(2,1)S(1)} %get-tuple-element.10), channel_id=1, source_target_pairs={{128,0},{192,64},{0,128},{64,192},{129,1},{193,65},{1,129},{65,193... | collective-permute-start | bytes 12296 | tf_op jit(solution)/shard_map/ppermute | solution.py:415
  24.2 0.1 collective-permute-start.5
  24.4 0.0 collective-permute-done.3
  24.4 1.9 %collective-permute-done.4 = bf16[16,128]{1,0:T(8,128)(2,1)S(1)} collective-permute-done((bf16[16,128]{1,0:T(8,128)(2,1)S(1)}, bf16[16,128]{1,0:T(8,128)(2,1)S(1)}, u32[]{:S(2)}, u32[]{:S(2)}) %collective-permute-start.4) | collective-permute-done | bytes 4128 | tf_op jit(solution)/shard_map/ppermute | solution.py:415
  26.3 1.0 %collective-permute-done.5 = bf16[16,128]{1,0:T(8,128)(2,1)S(1)} collective-permute-done((bf16[16,128]{1,0:T(8,128)(2,1)S(1)}, bf16[16,128]{1,0:T(8,128)(2,1)S(1)}, u32[]{:S(2)}, u32[]{:S(2)}) %collective-permute-start.5) | collective-permute-done | bytes 4128 | tf_op jit(solution)/shard_map/ppermute | solution.py:415
  27.3 11.1 %all-to-all-done = bf16[64,13,2,128]{3,2,1,0:T(2,128)(2,1)S(1)} async-done(((bf16[64,13,2,128]{3,2,1,0:T(2,128)(2,1)}), bf16[64,13,2,128]{3,2,1,0:T(2,128)(2,1)S(1)}, u32[]{:S(2)}, u32[]{:S(2)}) %all-to-all-start) | async-done | bytes 426016 | tf_op jit(solution)/shard_map/all_to_all | solution.py:400
  38.4 9.9 %shard_map.132 = bf16[1664,128]{1,0:T(8,128)(2,1)S(1)} custom-call(bf16[1664,128]{1,0:T(8,128)(2,1)S(1)} %bitcast.24, f32[3,192,192]{2,1,0:T(8,128)} %pot_hbm.1, bf16[512,512]{1,0:T(8,128)(2,1)} %constant.37.clone.yf_hbm, bf16[384,384]{1,0:T(8,128)(2,1)} %constant.38.clone.xf_hbm, bf16[384,384]{1,0:T(8,128)(2,1)} %constant.39.clone.xi_hbm, ...), custom_call_target="tpu_custom_call" | custom-call | tf_op jit(solution)/shard_map/pallas_call | solution.py:333
  48.3 0.1 copy_dynamic-update-slice_fusion
  48.4 22.1 %all_to_all.10 = bf16[64,13,2,128]{3,2,1,0:T(2,128)(2,1)S(1)} all-to-all(bf16[64,13,2,128]{3,2,1,0:T(2,128)(2,1)S(1)} %copy_dynamic-update-slice_fusion), channel_id=1, replica_groups=mesh['band'=4,'fft'=64] {'fft'}, dimensions={0} | all-to-all | bytes 851968 | tf_op jit(solution)/shard_map/all_to_all | solution.py:400
  70.5 6.0 %shard_map.134 = (bf16[4,2,4096]{2,1,0:T(2,128)(2,1)}, f32[2,4]{1,0:T(2,128)}) custom-call(bf16[1664,128]{1,0:T(8,128)(2,1)S(1)} %bitcast.26, bf16[4,2,4096]{2,1,0:T(2,128)(2,1)} %orb_hbm.3, s32[1,4096]{1,0:T(1,128)} %bitcast.28, s32[1,128]{1,0:T(1,128)} %bitcast.31, bf16[384,512]{1,0:T(8,128)(2,1)} %constant.41.clone.zi_hbm), custom_call_target="tpu_custom_call" | custom-call | tf_op jit(solution)/shard_map/pallas_call | solution.py:333
  (10 shorter events, 0.1 us)
Async XLA Ops:
  0.6 20.8 %collective-permute-start = (bf16[4,2,4096]{2,1,0:T(2,128)(2,1)}, bf16[4,2,4096]{2,1,0:T(2,128)(2,1)S(1)}, u32[]{:S(2)}, u32[]{:S(2)}) collective-permute-start(bf16[4,2,4096]{2,1,0:T(2,128)(2,1)} %refs_0_.1), channel_id=1, source_target_pairs={{0,64},{64,128},{128,192},{192,0},{1,65},{65,129},{129,193},{193,1... | collective-permute-start | bytes 196616 | tf_op jit(solution)/shard_map/ppermute | solution.py:413
  0.7 20.7 %collective-permute-start.1 = (bf16[4,2,4096]{2,1,0:T(2,128)(2,1)}, bf16[4,2,4096]{2,1,0:T(2,128)(2,1)S(1)}, u32[]{:S(2)}, u32[]{:S(2)}) collective-permute-start(bf16[4,2,4096]{2,1,0:T(2,128)(2,1)} %refs_0_.1), channel_id=1, source_target_pairs={{0,128},{64,192},{128,0},{192,64},{1,129},{65,193},{129,1},{193,65... | collective-permute-start | bytes 196616 | tf_op jit(solution)/shard_map/ppermute | solution.py:413
  3.0 18.4 %collective-permute-start.2 = (bf16[4,2,4096]{2,1,0:T(2,128)(2,1)}, bf16[4,2,4096]{2,1,0:T(2,128)(2,1)S(1)}, u32[]{:S(2)}, u32[]{:S(2)}) collective-permute-start(bf16[4,2,4096]{2,1,0:T(2,128)(2,1)} %refs_0_.1), channel_id=1, source_target_pairs={{0,192},{64,0},{128,64},{192,128},{1,193},{65,1},{129,65},{193,129... | collective-permute-start | bytes 196616 | tf_op jit(solution)/shard_map/ppermute | solution.py:413
  9.0 12.5 %copy-start = (bf16[16,2,4096]{2,1,0:T(2,128)(2,1)S(1)}, bf16[16,2,4096]{2,1,0:T(2,128)(2,1)}, u32[]{:S(2)}) copy-start(bf16[16,2,4096]{2,1,0:T(2,128)(2,1)} %sub_ref.1) | copy-start | bytes 786436
  9.0 12.5 %copy-start.1 = (bf16[4,2,4096]{2,1,0:T(2,128)(2,1)S(1)}, bf16[4,2,4096]{2,1,0:T(2,128)(2,1)}, u32[]{:S(2)}) copy-start(bf16[4,2,4096]{2,1,0:T(2,128)(2,1)} %refs_0_.1) | copy-start | bytes 196612
  9.0 29.4 %all-to-all-start = ((bf16[64,13,2,128]{3,2,1,0:T(2,128)(2,1)}), bf16[64,13,2,128]{3,2,1,0:T(2,128)(2,1)S(1)}, u32[]{:S(2)}, u32[]{:S(2)}) async-start(bf16[64,13,2,128]{3,2,1,0:T(2,128)(2,1)} %bitcast.2), calls=%async_computation | async-start | bytes 851968 | tf_op jit(solution)/shard_map/all_to_all | solution.py:400
  22.2 2.1 %collective-permute-start.3 = (bf16[16,128]{1,0:T(8,128)(2,1)S(1)}, bf16[16,128]{1,0:T(8,128)(2,1)S(1)}, u32[]{:S(2)}, u32[]{:S(2)}) collective-permute-start(bf16[16,128]{1,0:T(8,128)(2,1)S(1)} %get-tuple-element.9), channel_id=1, source_target_pairs={{64,0},{128,64},{192,128},{0,192},{65,1},{129,65},{193,129},{1,193... | collective-permute-start | bytes 12296 | tf_op jit(solution)/shard_map/ppermute | solution.py:415
  22.6 3.6 %collective-permute-start.4 = (bf16[16,128]{1,0:T(8,128)(2,1)S(1)}, bf16[16,128]{1,0:T(8,128)(2,1)S(1)}, u32[]{:S(2)}, u32[]{:S(2)}) collective-permute-start(bf16[16,128]{1,0:T(8,128)(2,1)S(1)} %get-tuple-element.10), channel_id=1, source_target_pairs={{128,0},{192,64},{0,128},{64,192},{129,1},{193,65},{1,129},{65,193... | collective-permute-start | bytes 12296 | tf_op jit(solution)/shard_map/ppermute | solution.py:415
  24.2 3.0 %collective-permute-start.5 = (bf16[16,128]{1,0:T(8,128)(2,1)S(1)}, bf16[16,128]{1,0:T(8,128)(2,1)S(1)}, u32[]{:S(2)}, u32[]{:S(2)}) collective-permute-start(bf16[16,128]{1,0:T(8,128)(2,1)S(1)} %get-tuple-element.11), channel_id=1, source_target_pairs={{192,0},{0,64},{64,128},{128,192},{193,1},{1,65},{65,129},{129,193... | collective-permute-start | bytes 12296 | tf_op jit(solution)/shard_map/ppermute | solution.py:415

commit v3 on v2

--- a/solution.py
+++ b/solution.py
@@ -21,6 +21,7 @@
 EXT = 2
 MSG = EXT + ROWS
 GRP = 16
+CUT = 512
 NT = (((1,), (1,)), ((), ()))
 TN = (((0,), (0,)), ((), ()))
 
@@ -48,19 +49,21 @@
         c, s = wide(c, N, width), wide(s * sign, N, width)
         return np.block([[c, -s], [s, c]])
 
-    def right(rows, cols, scale, sign, height, width):
+    def right(rows, cols, scale, sign, order, width):
         c, s = trig(rows, cols, scale)
-        c, s = wide(c, height, width), wide(s * sign, height, width)
-        return np.block([[c, s], [-s, c]])
-
+        c, s = wide(c, N, width), wide(s * sign, N, width)
+        full = np.block([[c, s], [-s, c]])
+        return full if order is None else full[np.ix_(order, order)]
+
+    packed = np.concatenate([np.arange(128), N + np.arange(128), np.arange(128, N), np.arange(N + 128, 2 * N)])
     inv = 1.0 / N
     out = {
         "zf": left(dealt, nat, 1.0, 1.0, W),
-        "yf": right(nat, nat, 1.0, 1.0, W, W),
+        "yf": right(nat, nat, 1.0, 1.0, packed, N),
         "xf": left(nat, dealt, 1.0, 1.0, N),
         "xi": left(dealt, nat, inv, -1.0, N),
-        "yi": right(nat, nat, inv, -1.0, W, W),
-        "zi": right(dealt, nat, inv, -1.0, N, W),
+        "yi": right(nat, nat, inv, -1.0, packed, N),
+        "zi": right(dealt, nat, inv, -1.0, None, W),
     }
     return {k: v.astype(np.float32).astype(BF) for k, v in out.items()}
 
@@ -135,7 +138,7 @@
 
 
 def plane_kernel(
-    in_ref, pot_hbm, yf_hbm, xf_hbm, xi_hbm, yi_hbm, out_ref, oh_scr, xl_scr, lo_scr, hi_scr, pot_scr, yf, xf, xi, yi, sems
+    in_ref, ext_ref, pot_hbm, yf_hbm, xf_hbm, xi_hbm, yi_hbm, out_ref, oh_scr, xl_scr, lo_scr, hi_scr, pot_scr, yf, xf, xi, yi, sems
 ):
     rows = ROWS
     copies = fetch(sems, (yf_hbm, yf), (xf_hbm, xf), (pot_hbm, pot_scr), (xi_hbm, xi), (yi_hbm, yi))
@@ -149,7 +152,7 @@
             xl, y = m[0:1], m[1:2].astype(jnp.int32)
             xl_scr[pl.ds(d, 1), :] = xl
             hot = jnp.where(iota((N, STK), 0) == y, 1.0, 0.0).astype(BF)
-            hot = jnp.concatenate([hot, jnp.zeros((W - N, STK), BF)], axis=0)
+            hot = jnp.concatenate([hot, hot[STK:]], axis=0)
             oh_scr[d] = hot
             lhs = jnp.concatenate([jnp.where(xl == k, m[EXT:], 0.0) for k in range(DEP)], axis=0).astype(BF)
             res = dot(lhs, hot, NT)
@@ -167,36 +170,45 @@
     for copy in copies:
         copy.wait()
 
+    left = iota((N, STK), 1) < STK // 2
+
+    def mixed(one, two):
+        return (
+            jnp.where(left, one, pltpu.roll(two, STK // 2, 1)),
+            jnp.where(left, pltpu.roll(one, STK // 2, 1), two),
+        )
+
     def plane(r, carry):
         at = r * 8 * N
         lined = []
         for b in range(4):
-            parts = [
-                half[pl.ds(at + 2 * b + p, N, stride=8), :].astype(BF) for p in range(2) for half in halves
-            ]
-            lined.append(jnp.concatenate(parts, axis=1))
-        ay = dot(jnp.concatenate(lined, axis=0), yf[...]).astype(BF).reshape(4, N, 2 * W)
-        stacked = jnp.concatenate(
-            [jnp.concatenate([ay[b, :, p * W : (p + 1) * W] for p in range(2)], axis=0) for b in range(4)], axis=1
-        )
-        ax = dot(xf[...], stacked)
-        pot = jnp.concatenate([pot_scr[r], jnp.zeros((N, W - N), F32)], axis=1)
-        pot = jnp.concatenate([jnp.concatenate([pot, pot], axis=0)] * 4, axis=1)
-        bx = dot(xi[...], (ax * pot).astype(BF)).astype(BF)
-        lined = jnp.concatenate(
-            [
-                jnp.concatenate([bx[p * N : (p + 1) * N, b * W : (b + 1) * W] for p in range(2)], axis=1)
-                for b in range(4)
-            ],
-            axis=0,
-        )
-        by = dot(lined, yi[...])
+            low = [lo_scr[pl.ds(at + 2 * b + p, N, stride=8), :] for p in range(2)]
+            high = [hi_scr[pl.ds(at + 2 * b + p, N, stride=8), :] for p in range(2)]
+            lined.append(jnp.concatenate([*low, jnp.where(left, *high)], axis=1).astype(BF))
+        ay = dot(jnp.concatenate(lined, axis=0), yf[...]).reshape(4, N, 2 * N)
+        blocks = [jnp.concatenate([ay[b, :, :STK], ay[b, :, STK : 2 * STK]], axis=0) for b in range(4)]
+        for b in range(0, 4, 2):
+            blocks.append(jnp.concatenate(mixed(ay[b, :, 2 * STK :], ay[b + 1, :, 2 * STK :]), axis=0))
+        ax = dot(xf[...], jnp.concatenate(blocks, axis=1).astype(BF))
+        pot = pot_scr[r]
+        pot = jnp.concatenate([pot[:, :STK]] * 4 + [pot[:, STK:]] * 4, axis=1)
+        pot = jnp.concatenate([pot, pot], axis=0)
+        bx = dot(xi[...], (ax * pot).astype(BF))
+        tails = []
+        for b in range(0, 4, 2):
+            cut = slice((4 + b // 2) * STK, (5 + b // 2) * STK)
+            tails += mixed(bx[:N, cut], bx[N:, cut])
+        lined = [
+            jnp.concatenate([bx[:N, b * STK : (b + 1) * STK], bx[N:, b * STK : (b + 1) * STK], tails[b]], axis=1)
+            for b in range(4)
+        ]
+        by = dot(jnp.concatenate(lined, axis=0).astype(BF), yi[...])
         for b in range(4):
+            part = by[b * N : (b + 1) * N]
+            high = part[:, 2 * STK :]
             for p in range(2):
-                for h in range(2):
-                    halves[h][pl.ds(at + 2 * b + p, N, stride=8), :] = by[
-                        b * N : (b + 1) * N, (2 * p + h) * STK : (2 * p + h + 1) * STK
-                    ]
+                lo_scr[pl.ds(at + 2 * b + p, N, stride=8), :] = part[:, p * STK : (p + 1) * STK]
+                hi_scr[pl.ds(at + 2 * b + p, N, stride=8), :] = jnp.where(left, *((high, 0.0) if p == 0 else (0.0, high)))
         return carry
 
     lax.fori_loop(0, DEP, plane, 0)
@@ -226,17 +238,41 @@
                     res[(t * DEP + k) * rows : (t * DEP + k + 1) * rows, t * STK : (t + 1) * STK] for k in range(DEP)
                 ]
                 field = jnp.where(xl == 0.0, took[0], jnp.where(xl == 1.0, took[1], took[2]))
-                parts += [jnp.zeros((EXT, STK), F32), field]
+                parts += [ext_ref[pl.ds(d, 1), :], jnp.zeros((EXT - 1, STK), F32), field]
         out_ref[pl.ds(pl.multiple_of(i * GRP * MSG, 16), GRP * MSG), :] = jnp.concatenate(parts, axis=0).astype(BF)
         return carry
 
     lax.fori_loop(0, OWN // GRP, gather, 0)
 
 
-def wave_kernel(
-    in_ref, orb_hbm, slot_hbm, col_hbm, zi_hbm, out_ref, sum_ref, m_scr, orb_ref, slot_ref, col_ref, zi_ref, sems
+def ready_kernel(
+    orb_hbm, slot_hbm, col_hbm, zi_hbm, hot_ref, base_ref, slot_ref, zi_ref, orb_ref, col_ref, sems
 ):
-    copies = fetch(sems, (zi_hbm, zi_ref), (col_hbm, col_ref), (slot_hbm, slot_ref), (orb_hbm, orb_ref))
+    copies = fetch(sems, (slot_hbm, slot_ref), (orb_hbm, orb_ref), (col_hbm, col_ref), (zi_hbm, zi_ref))
+    for copy in copies:
+        copy.wait()
+    x, y = column_coords(col_ref[...])
+    x = jnp.where(x >= N // 2, x - N, x)
+    y = jnp.where(y >= N // 2, y - N, y)
+    square = x * x + y * y
+    square = jnp.sum(jnp.where(iota((STK, STK), 0) == iota((STK, STK), 1), square, 0.0), axis=1, keepdims=True)
+
+    def step(i, carry):
+        cut = pl.ds(pl.multiple_of(i * CUT, CUT), CUT)
+        slot = slot_ref[:, cut]
+        z, stick = slot >> 7, slot & (STK - 1)
+        hot_ref[:, cut] = jnp.where(iota((N, CUT), 0) == z, 1.0, 0.0).astype(BF)
+        fz = jnp.where(z >= N // 2, z - N, z).astype(F32)
+        flat = jnp.sum(jnp.where(iota((STK, CUT), 0) == stick, square, 0.0), axis=0, keepdims=True)
+        kinetic = (fz * fz + flat) * (2.0 / (N * N))
+        for b in range(4):
+            base_ref[b, :, cut] = kinetic * orb_ref[b, :, cut].astype(F32)
+        return carry
+
+    lax.fori_loop(0, hot_ref.shape[1] // CUT, step, 0)
+
+
+def wave_kernel(in_ref, hot_ref, base_ref, slot_ref, zi_ref, out_ref, sum_ref, m_scr):
     npw = slot_ref.shape[1]
 
     def unpour(i, total):
@@ -255,57 +291,25 @@
     for b in range(4):
         picks = [m_scr[r, pl.ds(2 * b + p, OWN, stride=8), :] for p in range(2) for r in range(DEP)]
         cols.append(jnp.concatenate(picks, axis=0))
-    for copy in copies:
-        copy.wait()
     spectrum = jnp.concatenate(cols, axis=1).astype(BF)
     sticks = dot(spectrum, zi_ref[...], TN).astype(BF)
-    sticks = [
-        jnp.concatenate(
-            [
-                jnp.concatenate(
-                    [sticks[b * STK + 64 * h : b * STK + 64 * (h + 1), p * W : (p + 1) * W] for h in range(2)], axis=1
-                )
-                for b in range(4)
-            ],
-            axis=0,
-        )
-        for p in range(2)
-    ]
-    x, y = column_coords(col_ref[...])
-    x = jnp.where(x >= N // 2, x - N, x)
-    y = jnp.where(y >= N // 2, y - N, y)
-    square = x * x + y * y
-    square = jnp.sum(jnp.where(iota((STK, STK), 0) == iota((STK, STK), 1), square, 0.0), axis=1, keepdims=True)
-    half = 512
 
     def pick(i, carry):
-        at = pl.multiple_of(i * half, half)
-        slot = slot_ref[:, pl.ds(at, half)]
-        z = slot >> 7
-        stick = slot & (STK - 1)
-        hot = jnp.concatenate(
-            [jnp.where(iota((W, half), 0) == jnp.where(stick >> 6 == h, z, -1), 1.0, 0.0).astype(BF) for h in range(2)],
-            axis=0,
-        )
-        hit = iota((STK, half), 0) == stick
-        low = iota((64, half), 0) == (stick & 63)
-        fz = jnp.where(z >= N // 2, z - N, z).astype(F32)
-        kinetic = (fz * fz + jnp.sum(jnp.where(hit, square, 0.0), axis=0, keepdims=True)) * (2.0 / (N * N))
+        cut = pl.ds(pl.multiple_of(i * CUT, CUT), CUT)
+        hit = iota((STK, CUT), 0) == (slot_ref[:, cut] & (STK - 1))
+        hot = hot_ref[:, cut]
         lines = []
         for p in range(2):
-            res = dot(sticks[p], hot)
-            for b in range(4):
-                lines.append(jnp.sum(jnp.where(low, res[b * 64 : (b + 1) * 64], 0.0), axis=0, keepdims=True))
+            res = dot(sticks[:, p * W : p * W + N], hot)
+            lines.append(
+                [jnp.sum(jnp.where(hit, res[b * STK : (b + 1) * STK], 0.0), axis=0, keepdims=True) for b in range(4)]
+            )
         for b in range(4):
-            for p in range(2):
-                coeff = orb_ref[b, p : p + 1, pl.ds(at, half)].astype(F32)
-                lines[p * 4 + b] = lines[p * 4 + b] + kinetic * coeff
-        for b in range(4):
-            done = jnp.concatenate([lines[b], lines[4 + b]], axis=0)
-            out_ref[b, :, pl.ds(at, half)] = done.astype(BF)
-        return carry
-
-    lax.fori_loop(0, npw // half, pick, 0, unroll=2)
+            done = jnp.concatenate([lines[0][b], lines[1][b]], axis=0) + base_ref[b, :, cut]
+            out_ref[b, :, cut] = done.astype(BF)
+        return carry
+
+    lax.fori_loop(0, npw // CUT, pick, 0, unroll=2)
 
 
 def overlap_kernel(sub_ref, *refs):
@@ -328,14 +332,14 @@
         out_refs[k][...] = jnp.concatenate([top[:, cut], mid[:, cut], low[:, cut], pad], axis=1).astype(BF)
 
 
-def run(kernel, outs, scratch, args, near):
+def run(kernel, outs, scratch, args, near, room):
     space = [pltpu.VMEM if n else pltpu.HBM for n in near]
     return pl.pallas_call(
         kernel,
         out_shape=outs,
         in_specs=[pl.BlockSpec(memory_space=m) for m in space],
         scratch_shapes=scratch,
-        compiler_params=pltpu.CompilerParams(vmem_limit_bytes=52 << 20),
+        compiler_params=pltpu.CompilerParams(vmem_limit_bytes=room << 20),
     )(*[pltpu.with_memory_space_constraint(a, m) for a, m in zip(args, space)])
 
 
@@ -358,14 +362,15 @@
         ],
         args,
         (0, 0, 0, 0),
+        24,
     )
 
 
 def stage_over(sub, prevs):
-    return run(overlap_kernel, [pltpu.VMEM((16, STK), BF)] * 4, [], (sub, *prevs), (1, 1, 1, 1, 1))
-
-
-def stage_plane(got, pot):
+    return run(overlap_kernel, [pltpu.VMEM((16, STK), BF)] * 4, [], (sub, *prevs), (1, 1, 1, 1, 1), 8)
+
+
+def stage_plane(got, ext, pot):
     args = [jnp.asarray(tables()[k]) for k in ("yf", "xf", "xi", "yi")]
     return run(
         plane_kernel,
@@ -379,20 +384,32 @@
             *map(like, args),
             pltpu.SemaphoreType.DMA((5,)),
         ],
-        (got, pot, *args),
-        (1, 0, 0, 0, 0, 0),
+        (got, ext, pot, *args),
+        (1, 1, 0, 0, 0, 0, 0),
+        32,
     )
 
 
-def stage_wave(got, *args):
-    args = (*args, jnp.asarray(tables()["zi"]))
-    order = (args[0], args[1], args[2], args[3])
+def stage_ready(orb, slot, col):
+    args = (orb, slot, col, jnp.asarray(tables()["zi"]))
+    return run(
+        ready_kernel,
+        [pltpu.VMEM((N, slot.shape[1]), BF), pltpu.VMEM(orb.shape, F32), like(slot), like(args[3])],
+        [like(orb), like(col), pltpu.SemaphoreType.DMA((4,))],
+        args,
+        (0, 0, 0, 0),
+        12,
+    )
+
+
+def stage_wave(got, hot, base, slot, zi):
     return run(
         wave_kernel,
-        (jax.ShapeDtypeStruct(args[0].shape, BF), jax.ShapeDtypeStruct((2, 4), F32)),
-        [pltpu.VMEM((DEP, OWN * 8, STK), F32), *map(like, order), pltpu.SemaphoreType.DMA((len(args),))],
-        (got, *order),
-        (1, 0, 0, 0, 0),
+        (jax.ShapeDtypeStruct(base.shape, BF), jax.ShapeDtypeStruct((2, 4), F32)),
+        [pltpu.VMEM((DEP, OWN * 8, STK), F32)],
+        (got, hot, base, slot, zi),
+        (1, 1, 1, 1, 1),
+        16,
     )
 
 
@@ -407,18 +424,18 @@
     npw = sphere_slot.shape[0]
     slot = sphere_slot.reshape(1, npw)
     col = stick_column.reshape(1, STK)
+    shifts = [[(g, (g + k) % 4) for g in range(4)] for k in (1, 2, 3)]
+    others = [lax.ppermute(previous, "band", s) for s in shifts]
     send = stage_pack(orbitals, slot, col)
     got = exchange(send.reshape(TILES))
-    shifts = [[(g, (g + k) % 4) for g in range(4)] for k in (1, 2, 3)]
-    others = [lax.ppermute(previous, "band", s) for s in shifts]
     over = stage_over(subspace, [previous, *others])
     mine = [over[0]] + [lax.ppermute(over[k], "band", [(b, a) for a, b in shifts[k - 1]]) for k in (1, 2, 3)]
-    field = stage_plane(got, potential)
     sums = jnp.concatenate([jnp.stack(mine)] * 2)
-    sums = lax.dynamic_slice_in_dim(sums, (4 - lax.axis_index("band")) % 4, 4, 0).reshape(OWN, 1, STK)
-    head = jnp.pad(sums, ((0, 0), (0, 1), (0, 0)))[:, None]
-    back = exchange(lax.dynamic_update_slice(field.reshape(TILES), head, (0, 0, 0, 0)))
-    applied, total = stage_wave(back, orbitals, slot, col)
+    sums = lax.dynamic_slice_in_dim(sums, (4 - lax.axis_index("band")) % 4, 4, 0).reshape(OWN, STK)
+    prepared = stage_ready(orbitals, slot, col)
+    field = stage_plane(got, sums.astype(F32), potential)
+    back = exchange(field.reshape(TILES))
+    applied, total = stage_wave(back, *prepared)
     return applied, total.reshape(2, 1, 4)
 
 

time: 76.9 us -> 75.8 us (0.986)
  blocking collectives: 22.1 us -> 0 us
  waiting for transfers between devices: 14 us -> 28.5 us
  starting transfers between devices: 18.3 us -> 24.2 us
    all_to_all x1 -> x0, blocking collectives: 22.1 us -> none  [exchange(): lax.all_to_all(tiles, 'fft', 0, 0, tiled=True).reshape(OWN * MSG, STK)]
    all_to_all x1 -> x2, waiting for transfers between devices: 11.1 us -> 25.6 us  [exchange(): lax.all_to_all(tiles, 'fft', 0, 0, tiled=True).reshape(OWN * MSG, STK)]
    all_to_all x1 -> x2, starting transfers between devices: 12.4 us -> 18.1 us  [exchange(): lax.all_to_all(tiles, 'fft', 0, 0, tiled=True).reshape(OWN * MSG, STK)]
    pallas_call x4 -> x5, Pallas kernels: 21.3 us -> 21.9 us  [run(): pl.pallas_call(kernel, out_shape=outs, in_specs=[pl.BlockSpec(memory_spac...]
  transfers between devices with their start and end apart: 7 -> 8, of which waited for: 3 -> 4; matrix products, arithmetic and copies ran while one was open for 0% -> 0% of each run, Pallas kernels for 7% -> 10%
where the time goes in v3:
time: 75.8 us; the launch traced here: 75.5 us
  waiting for transfers between devices  28.5 us (38%)
  starting transfers between devices  24.2 us (32%)
  Pallas kernels  21.9 us (29%)
  between operations  0.77 us (1%)
    all_to_all x2, waiting for transfers between devices, exchange(): lax.all_to_all(tiles, 'fft', 0, 0, tiled=True).reshape(OWN * MSG, STK)  25.6 us
    pallas_call x5, Pallas kernels, run(): pl.pallas_call(kernel, out_shape=outs, in_specs=[pl.BlockSpec(memory_spac...  21.9 us
    all_to_all x2, starting transfers between devices, exchange(): lax.all_to_all(tiles, 'fft', 0, 0, tiled=True).reshape(OWN * MSG, STK)  18.1 us
    ppermute x3, starting transfers between devices, per_device(): others = [lax.ppermute(previous, 'band', s) for s in shifts]  4.07 us
    ppermute x3, waiting for transfers between devices, per_device(): lax.ppermute(over[k], 'band', [(b, a) for a, b in shifts[k - 1]])  2.88 us
    ppermute x3, starting transfers between devices, per_device(): lax.ppermute(over[k], 'band', [(b, a) for a, b in shifts[k - 1]])  2.11 us
  transfers between devices with their start and end apart: 8, of which 4 were waited for; matrix products, arithmetic and copies ran while one was open for 0% of the time, Pallas kernels for 10%

profile of v3, /device:TPU:2, one launch (start us, length us, event | category | flops | bytes accessed | tf_op | source)
XLA Modules:
  0.0 75.5 jit_solution(15408386369894592594)
XLA Ops:
  0.6 0.0 copy-start.1
  0.6 0.0 copy-start
  0.6 2.3 %collective-permute-start.1 = (bf16[4,2,4096]{2,1,0:T(2,128)(2,1)}, bf16[4,2,4096]{2,1,0:T(2,128)(2,1)S(1)}, u32[]{:S(2)}, u32[]{:S(2)}) collective-permute-start(bf16[4,2,4096]{2,1,0:T(2,128)(2,1)} %refs_0_.1), channel_id=1, source_target_pairs={{0,128},{64,192},{128,0},{192,64},{1,129},{65,193},{129,1},{193,65... | collective-permute-start | bytes 196616 | tf_op jit(solution)/shard_map/ppermute | solution.py:428
  3.0 0.0 collective-permute-start
  3.0 1.7 %collective-permute-start.2 = (bf16[4,2,4096]{2,1,0:T(2,128)(2,1)}, bf16[4,2,4096]{2,1,0:T(2,128)(2,1)S(1)}, u32[]{:S(2)}, u32[]{:S(2)}) collective-permute-start(bf16[4,2,4096]{2,1,0:T(2,128)(2,1)} %refs_0_.1), channel_id=1, source_target_pairs={{0,192},{64,0},{128,64},{192,128},{1,193},{65,1},{129,65},{193,129... | collective-permute-start | bytes 196616 | tf_op jit(solution)/shard_map/ppermute | solution.py:428
  4.7 4.6 %shard_map.131 = bf16[1664,128]{1,0:T(8,128)(2,1)} custom-call(bf16[4,2,4096]{2,1,0:T(2,128)(2,1)} %orb_hbm.3, s32[1,4096]{1,0:T(1,128)} %bitcast.26, s32[1,128]{1,0:T(1,128)} %bitcast.28, bf16[384,512]{1,0:T(8,128)(2,1)} %constant.34.clone.zf_hbm), custom_call_target="tpu_custom_call" | custom-call | tf_op jit(solution)/shard_map/pallas_call | solution.py:337
  9.3 12.3 %all-to-all-start = ((bf16[64,13,2,128]{3,2,1,0:T(2,128)(2,1)}), bf16[64,13,2,128]{3,2,1,0:T(2,128)(2,1)S(1)}, u32[]{:S(2)}, u32[]{:S(2)}) async-start(bf16[64,13,2,128]{3,2,1,0:T(2,128)(2,1)} %bitcast.2), calls=%async_computation | async-start | bytes 851968 | tf_op jit(solution)/shard_map/all_to_all | solution.py:417
  21.6 0.0 collective-permute-done.1.refs_2_
  21.6 0.0 collective-permute-done.refs_1_
  21.6 0.0 collective-permute-done.2.refs_3_
  21.6 0.0 copy-done.1
  21.6 0.0 copy-done
  21.6 0.8 %shard_map.132 = (bf16[16,128]{1,0:T(8,128)(2,1)S(1)}, bf16[16,128]{1,0:T(8,128)(2,1)S(1)}, bf16[16,128]{1,0:T(8,128)(2,1)S(1)}, bf16[16,128]{1,0:T(8,128)(2,1)S(1)}) custom-call(bf16[16,2,4096]{2,1,0:T(2,128)(2,1)S(1)} %copy-done, bf16[4,2,4096]{2,1,0:T(2,128)(2,1)S(1)} %copy-done.1, bf16[4,2,4096]{2,1,0:T(2,128)(2,1)S(1)} %collective-permute-done.refs_1_, ...), custom_call_target="tpu_custom_call" | custom-call | tf_op jit(solution)/shard_map/pallas_call | solution.py:337
  22.4 0.4 collective-permute-start.3
  22.8 1.6 %collective-permute-start.4 = (bf16[16,128]{1,0:T(8,128)(2,1)S(1)}, bf16[16,128]{1,0:T(8,128)(2,1)S(1)}, u32[]{:S(2)}, u32[]{:S(2)}) collective-permute-start(bf16[16,128]{1,0:T(8,128)(2,1)S(1)} %get-tuple-element.14), channel_id=1, source_target_pairs={{128,0},{192,64},{0,128},{64,192},{129,1},{193,65},{1,129},{65,193... | collective-permute-start | bytes 12296 | tf_op jit(solution)/shard_map/ppermute | solution.py:432
  24.4 0.1 collective-permute-start.5
  24.5 0.0 collective-permute-done.3
  24.5 1.9 %collective-permute-done.4 = bf16[16,128]{1,0:T(8,128)(2,1)S(1)} collective-permute-done((bf16[16,128]{1,0:T(8,128)(2,1)S(1)}, bf16[16,128]{1,0:T(8,128)(2,1)S(1)}, u32[]{:S(2)}, u32[]{:S(2)}) %collective-permute-start.4) | collective-permute-done | bytes 4128 | tf_op jit(solution)/shard_map/ppermute | solution.py:432
  26.4 1.0 %collective-permute-done.5 = bf16[16,128]{1,0:T(8,128)(2,1)S(1)} collective-permute-done((bf16[16,128]{1,0:T(8,128)(2,1)S(1)}, bf16[16,128]{1,0:T(8,128)(2,1)S(1)}, u32[]{:S(2)}, u32[]{:S(2)}) %collective-permute-start.5) | collective-permute-done | bytes 4128 | tf_op jit(solution)/shard_map/ppermute | solution.py:432
  27.5 11.1 %all-to-all-done = bf16[64,13,2,128]{3,2,1,0:T(2,128)(2,1)S(1)} async-done(((bf16[64,13,2,128]{3,2,1,0:T(2,128)(2,1)}), bf16[64,13,2,128]{3,2,1,0:T(2,128)(2,1)S(1)}, u32[]{:S(2)}, u32[]{:S(2)}) %all-to-all-start) | async-done | bytes 426016 | tf_op jit(solution)/shard_map/all_to_all | solution.py:417
  38.6 10.3 %shard_map.133 = bf16[1664,128]{1,0:T(8,128)(2,1)} custom-call(bf16[1664,128]{1,0:T(8,128)(2,1)S(1)} %bitcast.25, f32[64,128]{1,0:T(8,128)S(1)} %bitcast_convert_fusion.ext_ref, f32[3,192,192]{2,1,0:T(8,128)} %pot_hbm.1, bf16[384,384]{1,0:T(8,128)(2,1)} %constant.36.clone.yf_hbm, bf16[384,384]{1,0:T(8,128)(2,1)} %constant.37.clone.xf_hbm, ...), custom_call_target="tpu_custom_call" | custom-call | tf_op jit(solution)/shard_map/pallas_call | solution.py:337
  48.8 5.8 %all-to-all-start.1 = ((bf16[64,13,2,128]{3,2,1,0:T(2,128)(2,1)}), bf16[64,13,2,128]{3,2,1,0:T(2,128)(2,1)S(1)}, u32[]{:S(2)}, u32[]{:S(2)}) async-start(bf16[64,13,2,128]{3,2,1,0:T(2,128)(2,1)} %bitcast.9), calls=%async_computation.1 | async-start | bytes 851968 | tf_op jit(solution)/shard_map/all_to_all | solution.py:417
  54.6 2.0 %shard_map.134 = (bf16[192,4096]{1,0:T(8,128)(2,1)S(1)}, f32[4,2,4096]{2,1,0:T(2,128)S(1)}, s32[1,4096]{1,0:T(1,128)S(1)}, bf16[384,512]{1,0:T(8,128)(2,1)S(1)}) custom-call(bf16[4,2,4096]{2,1,0:T(2,128)(2,1)} %orb_hbm.3, s32[1,4096]{1,0:T(1,128)} %bitcast.27, s32[1,128]{1,0:T(1,128)} %bitcast.29, bf16[384,512]{1,0:T(8,128)(2,1)} %constant.35.clone.zi_hbm), custom_call_target="tpu_custom_call" | custom-call | tf_op jit(solution)/shard_map/pallas_call | solution.py:337
  56.6 14.6 %all-to-all-done.1 = bf16[64,13,2,128]{3,2,1,0:T(2,128)(2,1)S(1)} async-done(((bf16[64,13,2,128]{3,2,1,0:T(2,128)(2,1)}), bf16[64,13,2,128]{3,2,1,0:T(2,128)(2,1)S(1)}, u32[]{:S(2)}, u32[]{:S(2)}) %all-to-all-start.1) | async-done | bytes 426016 | tf_op jit(solution)/shard_map/all_to_all | solution.py:417
  71.2 4.3 %shard_map.135 = (bf16[4,2,4096]{2,1,0:T(2,128)(2,1)}, f32[2,4]{1,0:T(2,128)}) custom-call(bf16[1664,128]{1,0:T(8,128)(2,1)S(1)} %bitcast.24, bf16[192,4096]{1,0:T(8,128)(2,1)S(1)} %get-tuple-element.16.hot_ref, f32[4,2,4096]{2,1,0:T(2,128)S(1)} %get-tuple-element.17.base_ref, s32[1,4096]{1,0:T(1,128)S(1)} %get-tuple-element.18.slot_ref, ...), custom_call_target="tpu_custom_call" | custom-call | tf_op jit(solution)/shard_map/pallas_call | solution.py:337
  (10 shorter events, 0.1 us)
Async XLA Ops:
  0.6 21.0 %copy-start.1 = (bf16[4,2,4096]{2,1,0:T(2,128)(2,1)S(1)}, bf16[4,2,4096]{2,1,0:T(2,128)(2,1)}, u32[]{:S(2)}) copy-start(bf16[4,2,4096]{2,1,0:T(2,128)(2,1)} %refs_0_.1) | copy-start | bytes 196612
  0.6 21.0 %copy-start = (bf16[16,2,4096]{2,1,0:T(2,128)(2,1)S(1)}, bf16[16,2,4096]{2,1,0:T(2,128)(2,1)}, u32[]{:S(2)}) copy-start(bf16[16,2,4096]{2,1,0:T(2,128)(2,1)} %sub_ref.1) | copy-start | bytes 786436
  0.6 20.9 %collective-permute-start.1 = (bf16[4,2,4096]{2,1,0:T(2,128)(2,1)}, bf16[4,2,4096]{2,1,0:T(2,128)(2,1)S(1)}, u32[]{:S(2)}, u32[]{:S(2)}) collective-permute-start(bf16[4,2,4096]{2,1,0:T(2,128)(2,1)} %refs_0_.1), channel_id=1, source_target_pairs={{0,128},{64,192},{128,0},{192,64},{1,129},{65,193},{129,1},{193,65... | collective-permute-start | bytes 196616 | tf_op jit(solution)/shard_map/ppermute | solution.py:428
  3.0 18.6 %collective-permute-start = (bf16[4,2,4096]{2,1,0:T(2,128)(2,1)}, bf16[4,2,4096]{2,1,0:T(2,128)(2,1)S(1)}, u32[]{:S(2)}, u32[]{:S(2)}) collective-permute-start(bf16[4,2,4096]{2,1,0:T(2,128)(2,1)} %refs_0_.1), channel_id=1, source_target_pairs={{0,64},{64,128},{128,192},{192,0},{1,65},{65,129},{129,193},{193,1... | collective-permute-start | bytes 196616 | tf_op jit(solution)/shard_map/ppermute | solution.py:428
  3.0 18.6 %collective-permute-start.2 = (bf16[4,2,4096]{2,1,0:T(2,128)(2,1)}, bf16[4,2,4096]{2,1,0:T(2,128)(2,1)S(1)}, u32[]{:S(2)}, u32[]{:S(2)}) collective-permute-start(bf16[4,2,4096]{2,1,0:T(2,128)(2,1)} %refs_0_.1), channel_id=1, source_target_pairs={{0,192},{64,0},{128,64},{192,128},{1,193},{65,1},{129,65},{193,129... | collective-permute-start | bytes 196616 | tf_op jit(solution)/shard_map/ppermute | solution.py:428
  9.3 29.3 %all-to-all-start = ((bf16[64,13,2,128]{3,2,1,0:T(2,128)(2,1)}), bf16[64,13,2,128]{3,2,1,0:T(2,128)(2,1)S(1)}, u32[]{:S(2)}, u32[]{:S(2)}) async-start(bf16[64,13,2,128]{3,2,1,0:T(2,128)(2,1)} %bitcast.2), calls=%async_computation | async-start | bytes 851968 | tf_op jit(solution)/shard_map/all_to_all | solution.py:417
  22.4 2.1 %collective-permute-start.3 = (bf16[16,128]{1,0:T(8,128)(2,1)S(1)}, bf16[16,128]{1,0:T(8,128)(2,1)S(1)}, u32[]{:S(2)}, u32[]{:S(2)}) collective-permute-start(bf16[16,128]{1,0:T(8,128)(2,1)S(1)} %get-tuple-element.13), channel_id=1, source_target_pairs={{64,0},{128,64},{192,128},{0,192},{65,1},{129,65},{193,129},{1,193... | collective-permute-start | bytes 12296 | tf_op jit(solution)/shard_map/ppermute | solution.py:432
  22.8 3.6 %collective-permute-start.4 = (bf16[16,128]{1,0:T(8,128)(2,1)S(1)}, bf16[16,128]{1,0:T(8,128)(2,1)S(1)}, u32[]{:S(2)}, u32[]{:S(2)}) collective-permute-start(bf16[16,128]{1,0:T(8,128)(2,1)S(1)} %get-tuple-element.14), channel_id=1, source_target_pairs={{128,0},{192,64},{0,128},{64,192},{129,1},{193,65},{1,129},{65,193... | collective-permute-start | bytes 12296 | tf_op jit(solution)/shard_map/ppermute | solution.py:432
  24.4 3.0 %collective-permute-start.5 = (bf16[16,128]{1,0:T(8,128)(2,1)S(1)}, bf16[16,128]{1,0:T(8,128)(2,1)S(1)}, u32[]{:S(2)}, u32[]{:S(2)}) collective-permute-start(bf16[16,128]{1,0:T(8,128)(2,1)S(1)} %get-tuple-element.15), channel_id=1, source_target_pairs={{192,0},{0,64},{64,128},{128,192},{193,1},{1,65},{65,129},{129,193... | collective-permute-start | bytes 12296 | tf_op jit(solution)/shard_map/ppermute | solution.py:432
  48.8 22.4 %all-to-all-start.1 = ((bf16[64,13,2,128]{3,2,1,0:T(2,128)(2,1)}), bf16[64,13,2,128]{3,2,1,0:T(2,128)(2,1)S(1)}, u32[]{:S(2)}, u32[]{:S(2)}) async-start(bf16[64,13,2,128]{3,2,1,0:T(2,128)(2,1)} %bitcast.9), calls=%async_computation.1 | async-start | bytes 851968 | tf_op jit(solution)/shard_map/all_to_all | solution.py:417

commit v4 on v3

--- a/solution.py
+++ b/solution.py
@@ -86,7 +86,7 @@
 
 
 def pack_kernel(
-    orb_hbm, slot_hbm, col_hbm, zf_hbm, out_ref, a_scr, b_scr, m_scr, orb_ref, slot_ref, col_ref, zf_ref, sems
+    orb_hbm, slot_hbm, col_hbm, zf_hbm, out_hbm, a_scr, b_scr, m_scr, out_ref, orb_ref, slot_ref, col_ref, zf_ref, sems
 ):
     copies = fetch(sems, (slot_hbm, slot_ref), (orb_hbm, orb_ref), (col_hbm, col_ref), (zf_hbm, zf_ref))
     npw = slot_ref.shape[1]
@@ -125,20 +125,21 @@
             base = (j % 2) * N + r * OWN
             m_scr[r, pl.ds(j, OWN, stride=8), :] = wave[base : base + OWN, STK * (j // 2) : STK * (j // 2 + 1)]
 
-    def pour(i, carry):
-        at = pl.multiple_of(i * GRP * 8, 8)
-        block = [m_scr[r, pl.ds(at, GRP * 8), :] for r in range(DEP)]
+    copies = []
+    for i in range(OWN // GRP):
         parts = []
-        for u in range(GRP):
-            parts += [ext] + [block[r][8 * u : 8 * u + 8] for r in range(DEP)]
-        out_ref[pl.ds(pl.multiple_of(i * GRP * MSG, 16), GRP * MSG), :] = jnp.concatenate(parts, axis=0).astype(BF)
-        return carry
-
-    lax.fori_loop(0, OWN // GRP, pour, 0)
+        for u in range(i * GRP, (i + 1) * GRP):
+            parts += [ext] + [m_scr[r, 8 * u : 8 * u + 8] for r in range(DEP)]
+        cut = pl.ds(i * GRP * MSG, GRP * MSG)
+        out_ref[cut, :] = jnp.concatenate(parts, axis=0).astype(BF)
+        copies.append(pltpu.make_async_copy(out_ref.at[cut], out_hbm.at[cut], sems.at[4 + i]))
+        copies[-1].start()
+    for copy in copies:
+        copy.wait()
 
 
 def plane_kernel(
-    in_ref, ext_ref, pot_hbm, yf_hbm, xf_hbm, xi_hbm, yi_hbm, out_ref, oh_scr, xl_scr, lo_scr, hi_scr, pot_scr, yf, xf, xi, yi, sems
+    in_ref, pot_hbm, yf_hbm, xf_hbm, xi_hbm, yi_hbm, out_ref, oh_scr, xl_scr, lo_scr, hi_scr, pot_scr, yf, xf, xi, yi, sems
 ):
     rows = ROWS
     copies = fetch(sems, (yf_hbm, yf), (xf_hbm, xf), (pot_hbm, pot_scr), (xi_hbm, xi), (yi_hbm, yi))
@@ -238,7 +239,7 @@
                     res[(t * DEP + k) * rows : (t * DEP + k + 1) * rows, t * STK : (t + 1) * STK] for k in range(DEP)
                 ]
                 field = jnp.where(xl == 0.0, took[0], jnp.where(xl == 1.0, took[1], took[2]))
-                parts += [ext_ref[pl.ds(d, 1), :], jnp.zeros((EXT - 1, STK), F32), field]
+                parts += [jnp.zeros((EXT, STK), F32), field]
         out_ref[pl.ds(pl.multiple_of(i * GRP * MSG, 16), GRP * MSG), :] = jnp.concatenate(parts, axis=0).astype(BF)
         return carry
 
@@ -332,12 +333,13 @@
         out_refs[k][...] = jnp.concatenate([top[:, cut], mid[:, cut], low[:, cut], pad], axis=1).astype(BF)
 
 
-def run(kernel, outs, scratch, args, near, room):
+def run(kernel, outs, scratch, args, near, room, to=None):
     space = [pltpu.VMEM if n else pltpu.HBM for n in near]
     return pl.pallas_call(
         kernel,
         out_shape=outs,
         in_specs=[pl.BlockSpec(memory_space=m) for m in space],
+        **({} if to is None else {"out_specs": pl.BlockSpec(memory_space=to)}),
         scratch_shapes=scratch,
         compiler_params=pltpu.CompilerParams(vmem_limit_bytes=room << 20),
     )(*[pltpu.with_memory_space_constraint(a, m) for a, m in zip(args, space)])
@@ -352,17 +354,19 @@
     npw = args[1].shape[1]
     return run(
         pack_kernel,
-        pltpu.VMEM((OWN * MSG, STK), BF),
+        pltpu.HBM((OWN * MSG, STK), BF),
         [
             pltpu.VMEM((2 * W, npw), BF),
             pltpu.VMEM((512, npw), BF),
             pltpu.VMEM((DEP, OWN * 8, STK), F32),
+            pltpu.VMEM((OWN * MSG, STK), BF),
             *map(like, args),
-            pltpu.SemaphoreType.DMA((len(args),)),
+            pltpu.SemaphoreType.DMA((4 + OWN // GRP,)),
         ],
         args,
         (0, 0, 0, 0),
         24,
+        pltpu.HBM,
     )
 
 
@@ -370,7 +374,7 @@
     return run(overlap_kernel, [pltpu.VMEM((16, STK), BF)] * 4, [], (sub, *prevs), (1, 1, 1, 1, 1), 8)
 
 
-def stage_plane(got, ext, pot):
+def stage_plane(got, pot):
     args = [jnp.asarray(tables()[k]) for k in ("yf", "xf", "xi", "yi")]
     return run(
         plane_kernel,
@@ -384,8 +388,8 @@
             *map(like, args),
             pltpu.SemaphoreType.DMA((5,)),
         ],
-        (got, ext, pot, *args),
-        (1, 1, 0, 0, 0, 0, 0),
+        (got, pot, *args),
+        (1, 0, 0, 0, 0, 0),
         32,
     )
 
@@ -424,17 +428,24 @@
     npw = sphere_slot.shape[0]
     slot = sphere_slot.reshape(1, npw)
     col = stick_column.reshape(1, STK)
-    shifts = [[(g, (g + k) % 4) for g in range(4)] for k in (1, 2, 3)]
-    others = [lax.ppermute(previous, "band", s) for s in shifts]
+
+    def swapped(a, k):
+        return lax.ppermute(a, "band", [(g, g ^ k) for g in range(4)])
+
+    beside = swapped(previous, 1)
     send = stage_pack(orbitals, slot, col)
     got = exchange(send.reshape(TILES))
+    others = [beside, swapped(previous, 2), swapped(beside, 2)]
     over = stage_over(subspace, [previous, *others])
-    mine = [over[0]] + [lax.ppermute(over[k], "band", [(b, a) for a, b in shifts[k - 1]]) for k in (1, 2, 3)]
-    sums = jnp.concatenate([jnp.stack(mine)] * 2)
-    sums = lax.dynamic_slice_in_dim(sums, (4 - lax.axis_index("band")) % 4, 4, 0).reshape(OWN, STK)
+    mine = [over[0]] + [swapped(over[k], k) for k in (1, 2, 3)]
     prepared = stage_ready(orbitals, slot, col)
-    field = stage_plane(got, sums.astype(F32), potential)
-    back = exchange(field.reshape(TILES))
+    field = stage_plane(got, potential)
+    group = lax.axis_index("band")
+    for k in (1, 2):
+        mine = [jnp.where((group & k) > 0, mine[i ^ k], mine[i]) for i in range(4)]
+    sums = jnp.concatenate(mine, axis=0).reshape(OWN, 1, 1, STK)
+    head = jnp.pad(sums, ((0, 0), (0, 0), (0, EXT - 1), (0, 0)))
+    back = exchange(lax.dynamic_update_slice(field.reshape(TILES), head, (0, 0, 0, 0)))
     applied, total = stage_wave(back, *prepared)
     return applied, total.reshape(2, 1, 4)
 

time: 75.8 us -> 77.3 us (1.020)
  starting transfers between devices: 24.2 us -> 26.8 us
  waiting for transfers between devices: 28.5 us -> 26.7 us
    all_to_all x2, waiting for transfers between devices: 25.6 us -> 19 us  [exchange(): lax.all_to_all(tiles, 'fft', 0, 0, tiled=True).reshape(OWN * MSG, STK)]
    ppermute x6, waiting for transfers between devices: 2.89 us -> 7.69 us  [swapped(): return lax.ppermute(a, 'band', [(g, g ^ k) for g in range(4)])]
    all_to_all x2, starting transfers between devices: 18.1 us -> 22 us  [exchange(): lax.all_to_all(tiles, 'fft', 0, 0, tiled=True).reshape(OWN * MSG, STK)]
    ppermute x6, starting transfers between devices: 6.18 us -> 4.71 us  [swapped(): return lax.ppermute(a, 'band', [(g, g ^ k) for g in range(4)])]
  transfers between devices with their start and end apart: 8 -> 8, of which waited for: 4 -> 6; matrix products, arithmetic and copies ran while one was open for 0% -> 0% of each run, Pallas kernels for 10% -> 4%
where the time goes in v4:
time: 77.3 us; the launch traced here: 76.7 us
  starting transfers between devices  26.8 us (35%)
  waiting for transfers between devices  26.7 us (35%)
  Pallas kernels  21.8 us (28%)
    all_to_all x2, starting transfers between devices, exchange(): lax.all_to_all(tiles, 'fft', 0, 0, tiled=True).reshape(OWN * MSG, STK)  22 us
    pallas_call x5, Pallas kernels, run(): pl.pallas_call(kernel, out_shape=outs, in_specs=[pl.BlockSpec(memory_spac...  21.8 us
    all_to_all x2, waiting for transfers between devices, exchange(): lax.all_to_all(tiles, 'fft', 0, 0, tiled=True).reshape(OWN * MSG, STK)  19 us
    ppermute x6, waiting for transfers between devices, swapped(): return lax.ppermute(a, 'band', [(g, g ^ k) for g in range(4)])  7.69 us
    ppermute x6, starting transfers between devices, swapped(): return lax.ppermute(a, 'band', [(g, g ^ k) for g in range(4)])  4.71 us
  transfers between devices with their start and end apart: 8, of which 6 were waited for; matrix products, arithmetic and copies ran while one was open for 0% of the time, Pallas kernels for 4%

profile of v4, /device:TPU:2, one launch (start us, length us, event | category | flops | bytes accessed | tf_op | source)
XLA Modules:
  0.0 76.7 jit_solution(9257879299113927291)
XLA Ops:
  0.6 0.0 copy-start.1
  0.6 0.0 copy-start
  0.6 4.6 %shard_map.131 = bf16[1664,128]{1,0:T(8,128)(2,1)} custom-call(bf16[4,2,4096]{2,1,0:T(2,128)(2,1)} %orb_hbm.3, s32[1,4096]{1,0:T(1,128)} %bitcast.14, s32[1,128]{1,0:T(1,128)} %bitcast.16, bf16[384,512]{1,0:T(8,128)(2,1)} %constant.26.clone.zf_hbm), custom_call_target="tpu_custom_call" | custom-call | tf_op jit(solution)/shard_map/pallas_call | solution.py:338
  5.3 13.7 %all-to-all-start = ((bf16[64,13,2,128]{3,2,1,0:T(2,128)(2,1)}), bf16[64,13,2,128]{3,2,1,0:T(2,128)(2,1)S(1)}, u32[]{:S(2)}, u32[]{:S(2)}) async-start(bf16[64,13,2,128]{3,2,1,0:T(2,128)(2,1)} %bitcast.13), calls=%async_computation | async-start | bytes 851968 | tf_op jit(solution)/shard_map/all_to_all | solution.py:421
  18.9 0.0 copy-done.1
  19.0 0.1 collective-permute-start
  19.1 1.5 %collective-permute-start.1 = (bf16[4,2,4096]{2,1,0:T(2,128)(2,1)S(1)}, bf16[4,2,4096]{2,1,0:T(2,128)(2,1)S(1)}, u32[]{:S(2)}, u32[]{:S(2)}) collective-permute-start(bf16[4,2,4096]{2,1,0:T(2,128)(2,1)S(1)} %copy-done.1), channel_id=1, source_target_pairs={{0,128},{64,192},{128,0},{192,64},{1,129},{65,193},{129,1},{193,65... | collective-permute-start | bytes 196616 | tf_op jit(solution)/shard_map/ppermute | solution.py:433
  20.6 0.0 collective-permute-done.refs_1_
  20.6 1.2 %collective-permute-start.2 = (bf16[4,2,4096]{2,1,0:T(2,128)(2,1)S(1)}, bf16[4,2,4096]{2,1,0:T(2,128)(2,1)S(1)}, u32[]{:S(2)}, u32[]{:S(2)}) collective-permute-start(bf16[4,2,4096]{2,1,0:T(2,128)(2,1)S(1)} %collective-permute-done.refs_1_), channel_id=1, source_target_pairs={{0,128},{64,192},{128,0},{192,64},{1,129},{65,193},{129,1},{193,65... | collective-permute-start | bytes 196616 | tf_op jit(solution)/shard_map/ppermute | solution.py:433
  21.7 3.4 %collective-permute-done.1.refs_2_ = bf16[4,2,4096]{2,1,0:T(2,128)(2,1)S(1)} collective-permute-done((bf16[4,2,4096]{2,1,0:T(2,128)(2,1)S(1)}, bf16[4,2,4096]{2,1,0:T(2,128)(2,1)S(1)}, u32[]{:S(2)}, u32[]{:S(2)}) %collective-permute-start.1) | collective-permute-done | bytes 65568 | tf_op jit(solution)/shard_map/ppermute | solution.py:433
  25.1 1.7 %collective-permute-done.2.refs_3_ = bf16[4,2,4096]{2,1,0:T(2,128)(2,1)S(1)} collective-permute-done((bf16[4,2,4096]{2,1,0:T(2,128)(2,1)S(1)}, bf16[4,2,4096]{2,1,0:T(2,128)(2,1)S(1)}, u32[]{:S(2)}, u32[]{:S(2)}) %collective-permute-start.2) | collective-permute-done | bytes 65568 | tf_op jit(solution)/shard_map/ppermute | solution.py:433
  26.8 0.0 copy-done
  26.8 0.8 %shard_map.133 = (bf16[16,128]{1,0:T(8,128)(2,1)S(1)}, bf16[16,128]{1,0:T(8,128)(2,1)S(1)}, bf16[16,128]{1,0:T(8,128)(2,1)S(1)}, bf16[16,128]{1,0:T(8,128)(2,1)S(1)}) custom-call(bf16[16,2,4096]{2,1,0:T(2,128)(2,1)S(1)} %copy-done, bf16[4,2,4096]{2,1,0:T(2,128)(2,1)S(1)} %copy-done.1, bf16[4,2,4096]{2,1,0:T(2,128)(2,1)S(1)} %collective-permute-done.refs_1_, ...), custom_call_target="tpu_custom_call" | custom-call | tf_op jit(solution)/shard_map/pallas_call | solution.py:338
  27.6 1.0 %collective-permute-start.3 = (bf16[16,128]{1,0:T(8,128)(2,1)S(1)}, bf16[16,128]{1,0:T(8,128)(2,1)S(1)}, u32[]{:S(2)}, u32[]{:S(2)}) collective-permute-start(bf16[16,128]{1,0:T(8,128)(2,1)S(1)} %get-tuple-element.12), channel_id=1, source_target_pairs={{0,192},{64,128},{128,64},{192,0},{1,193},{65,129},{129,65},{193,1... | collective-permute-start | bytes 12296 | tf_op jit(solution)/shard_map/ppermute | solution.py:433
  28.5 0.8 %collective-permute-start.4 = (bf16[16,128]{1,0:T(8,128)(2,1)S(1)}, bf16[16,128]{1,0:T(8,128)(2,1)S(1)}, u32[]{:S(2)}, u32[]{:S(2)}) collective-permute-start(bf16[16,128]{1,0:T(8,128)(2,1)S(1)} %get-tuple-element.13), channel_id=1, source_target_pairs={{0,128},{64,192},{128,0},{192,64},{1,129},{65,193},{129,1},{193,65... | collective-permute-start | bytes 12296 | tf_op jit(solution)/shard_map/ppermute | solution.py:433
  29.4 0.2 collective-permute-start.5
  29.5 1.2 %collective-permute-done.3 = bf16[16,128]{1,0:T(8,128)(2,1)S(1)} collective-permute-done((bf16[16,128]{1,0:T(8,128)(2,1)S(1)}, bf16[16,128]{1,0:T(8,128)(2,1)S(1)}, u32[]{:S(2)}, u32[]{:S(2)}) %collective-permute-start.3) | collective-permute-done | bytes 4128 | tf_op jit(solution)/shard_map/ppermute | solution.py:433
  30.7 1.4 %collective-permute-done.4 = bf16[16,128]{1,0:T(8,128)(2,1)S(1)} collective-permute-done((bf16[16,128]{1,0:T(8,128)(2,1)S(1)}, bf16[16,128]{1,0:T(8,128)(2,1)S(1)}, u32[]{:S(2)}, u32[]{:S(2)}) %collective-permute-start.4) | collective-permute-done | bytes 4128 | tf_op jit(solution)/shard_map/ppermute | solution.py:433
  32.2 0.0 collective-permute-done.5
  32.2 4.0 %all-to-all-done = bf16[64,13,2,128]{3,2,1,0:T(2,128)(2,1)S(1)} async-done(((bf16[64,13,2,128]{3,2,1,0:T(2,128)(2,1)}), bf16[64,13,2,128]{3,2,1,0:T(2,128)(2,1)S(1)}, u32[]{:S(2)}, u32[]{:S(2)}) %all-to-all-start) | async-done | bytes 426016 | tf_op jit(solution)/shard_map/all_to_all | solution.py:421
  36.2 10.2 %shard_map.132 = bf16[1664,128]{1,0:T(8,128)(2,1)} custom-call(bf16[1664,128]{1,0:T(8,128)(2,1)S(1)} %bitcast.11, f32[3,192,192]{2,1,0:T(8,128)} %pot_hbm.1, bf16[384,384]{1,0:T(8,128)(2,1)} %constant.28.clone.yf_hbm, bf16[384,384]{1,0:T(8,128)(2,1)} %constant.29.clone.xf_hbm, bf16[384,384]{1,0:T(8,128)(2,1)} %constant.30.clone.xi_hbm, ...), custom_call_target="tpu_custom_call" | custom-call | tf_op jit(solution)/shard_map/pallas_call | solution.py:338
  46.4 0.7 pad_dynamic-update-slice_fusion
  47.1 8.4 %all-to-all-start.1 = ((bf16[64,13,2,128]{3,2,1,0:T(2,128)(2,1)}), bf16[64,13,2,128]{3,2,1,0:T(2,128)(2,1)S(1)}, u32[]{:S(2)}, u32[]{:S(2)}) async-start(bf16[64,13,2,128]{3,2,1,0:T(2,128)(2,1)} %pad_dynamic-update-slice_fusion), calls=%async_computation.1 | async-start | bytes 851968 | tf_op jit(solution)/shard_map/all_to_all | solution.py:421
  55.4 2.0 %shard_map.134 = (bf16[192,4096]{1,0:T(8,128)(2,1)S(1)}, f32[4,2,4096]{2,1,0:T(2,128)S(1)}, s32[1,4096]{1,0:T(1,128)S(1)}, bf16[384,512]{1,0:T(8,128)(2,1)S(1)}) custom-call(bf16[4,2,4096]{2,1,0:T(2,128)(2,1)} %orb_hbm.3, s32[1,4096]{1,0:T(1,128)} %bitcast.15, s32[1,128]{1,0:T(1,128)} %bitcast.17, bf16[384,512]{1,0:T(8,128)(2,1)} %constant.27.clone.zi_hbm), custom_call_target="tpu_custom_call" | custom-call | tf_op jit(solution)/shard_map/pallas_call | solution.py:338
  57.4 15.0 %all-to-all-done.1 = bf16[64,13,2,128]{3,2,1,0:T(2,128)(2,1)S(1)} async-done(((bf16[64,13,2,128]{3,2,1,0:T(2,128)(2,1)}), bf16[64,13,2,128]{3,2,1,0:T(2,128)(2,1)S(1)}, u32[]{:S(2)}, u32[]{:S(2)}) %all-to-all-start.1) | async-done | bytes 426016 | tf_op jit(solution)/shard_map/all_to_all | solution.py:421
  72.5 4.3 %shard_map.135 = (bf16[4,2,4096]{2,1,0:T(2,128)(2,1)}, f32[2,4]{1,0:T(2,128)}) custom-call(bf16[1664,128]{1,0:T(8,128)(2,1)S(1)} %bitcast.12, bf16[192,4096]{1,0:T(8,128)(2,1)S(1)} %get-tuple-element.16.hot_ref, f32[4,2,4096]{2,1,0:T(2,128)S(1)} %get-tuple-element.17.base_ref, s32[1,4096]{1,0:T(1,128)S(1)} %get-tuple-element.18.slot_ref, ...), custom_call_target="tpu_custom_call" | custom-call | tf_op jit(solution)/shard_map/pallas_call | solution.py:338
  (3 shorter events, 0.0 us)
Async XLA Ops:
  0.6 18.3 %copy-start.1 = (bf16[4,2,4096]{2,1,0:T(2,128)(2,1)S(1)}, bf16[4,2,4096]{2,1,0:T(2,128)(2,1)}, u32[]{:S(2)}) copy-start(bf16[4,2,4096]{2,1,0:T(2,128)(2,1)} %refs_0_.1) | copy-start | bytes 196612
  0.6 26.2 %copy-start = (bf16[16,2,4096]{2,1,0:T(2,128)(2,1)S(1)}, bf16[16,2,4096]{2,1,0:T(2,128)(2,1)}, u32[]{:S(2)}) copy-start(bf16[16,2,4096]{2,1,0:T(2,128)(2,1)} %sub_ref.1) | copy-start | bytes 786436
  5.3 30.9 %all-to-all-start = ((bf16[64,13,2,128]{3,2,1,0:T(2,128)(2,1)}), bf16[64,13,2,128]{3,2,1,0:T(2,128)(2,1)S(1)}, u32[]{:S(2)}, u32[]{:S(2)}) async-start(bf16[64,13,2,128]{3,2,1,0:T(2,128)(2,1)} %bitcast.13), calls=%async_computation | async-start | bytes 851968 | tf_op jit(solution)/shard_map/all_to_all | solution.py:421
  19.0 1.6 %collective-permute-start = (bf16[4,2,4096]{2,1,0:T(2,128)(2,1)S(1)}, bf16[4,2,4096]{2,1,0:T(2,128)(2,1)S(1)}, u32[]{:S(2)}, u32[]{:S(2)}) collective-permute-start(bf16[4,2,4096]{2,1,0:T(2,128)(2,1)S(1)} %copy-done.1), channel_id=1, source_target_pairs={{0,64},{64,0},{128,192},{192,128},{1,65},{65,1},{129,193},{193,129... | collective-permute-start | bytes 196616 | tf_op jit(solution)/shard_map/ppermute | solution.py:433
  19.1 6.0 %collective-permute-start.1 = (bf16[4,2,4096]{2,1,0:T(2,128)(2,1)S(1)}, bf16[4,2,4096]{2,1,0:T(2,128)(2,1)S(1)}, u32[]{:S(2)}, u32[]{:S(2)}) collective-permute-start(bf16[4,2,4096]{2,1,0:T(2,128)(2,1)S(1)} %copy-done.1), channel_id=1, source_target_pairs={{0,128},{64,192},{128,0},{192,64},{1,129},{65,193},{129,1},{193,65... | collective-permute-start | bytes 196616 | tf_op jit(solution)/shard_map/ppermute | solution.py:433
  20.6 6.2 %collective-permute-start.2 = (bf16[4,2,4096]{2,1,0:T(2,128)(2,1)S(1)}, bf16[4,2,4096]{2,1,0:T(2,128)(2,1)S(1)}, u32[]{:S(2)}, u32[]{:S(2)}) collective-permute-start(bf16[4,2,4096]{2,1,0:T(2,128)(2,1)S(1)} %collective-permute-done.refs_1_), channel_id=1, source_target_pairs={{0,128},{64,192},{128,0},{192,64},{1,129},{65,193},{129,1},{193,65... | collective-permute-start | bytes 196616 | tf_op jit(solution)/shard_map/ppermute | solution.py:433
  27.6 3.1 %collective-permute-start.3 = (bf16[16,128]{1,0:T(8,128)(2,1)S(1)}, bf16[16,128]{1,0:T(8,128)(2,1)S(1)}, u32[]{:S(2)}, u32[]{:S(2)}) collective-permute-start(bf16[16,128]{1,0:T(8,128)(2,1)S(1)} %get-tuple-element.12), channel_id=1, source_target_pairs={{0,192},{64,128},{128,64},{192,0},{1,193},{65,129},{129,65},{193,1... | collective-permute-start | bytes 12296 | tf_op jit(solution)/shard_map/ppermute | solution.py:433
  28.5 3.6 %collective-permute-start.4 = (bf16[16,128]{1,0:T(8,128)(2,1)S(1)}, bf16[16,128]{1,0:T(8,128)(2,1)S(1)}, u32[]{:S(2)}, u32[]{:S(2)}) collective-permute-start(bf16[16,128]{1,0:T(8,128)(2,1)S(1)} %get-tuple-element.13), channel_id=1, source_target_pairs={{0,128},{64,192},{128,0},{192,64},{1,129},{65,193},{129,1},{193,65... | collective-permute-start | bytes 12296 | tf_op jit(solution)/shard_map/ppermute | solution.py:433
  29.4 2.8 %collective-permute-start.5 = (bf16[16,128]{1,0:T(8,128)(2,1)S(1)}, bf16[16,128]{1,0:T(8,128)(2,1)S(1)}, u32[]{:S(2)}, u32[]{:S(2)}) collective-permute-start(bf16[16,128]{1,0:T(8,128)(2,1)S(1)} %get-tuple-element.14), channel_id=1, source_target_pairs={{0,64},{64,0},{128,192},{192,128},{1,65},{65,1},{129,193},{193,129... | collective-permute-start | bytes 12296 | tf_op jit(solution)/shard_map/ppermute | solution.py:433
  47.1 25.4 %all-to-all-start.1 = ((bf16[64,13,2,128]{3,2,1,0:T(2,128)(2,1)}), bf16[64,13,2,128]{3,2,1,0:T(2,128)(2,1)S(1)}, u32[]{:S(2)}, u32[]{:S(2)}) async-start(bf16[64,13,2,128]{3,2,1,0:T(2,128)(2,1)} %pad_dynamic-update-slice_fusion), calls=%async_computation.1 | async-start | bytes 851968 | tf_op jit(solution)/shard_map/all_to_all | solution.py:421
